TPU v7x, 32 devices: a whole 2x2x4 slice. The times are simulated.
32 devices in a mesh: box: 16 (over z, y, core), lev: 2 (over x).
Axes of the slice: x: 2, y: 2, z: 4, core: 2. Of those that a mesh axis runs over, the one named last changes fastest.
Arguments:
- fine: float32 [96, 5, 32, 1024], P(('box', 'lev')), may hold values from -12 to 12
- coarse: float32 [5, 256, 32, 128], P(None, 'box', 'lev'), may hold values from -6 to 6
- owner_map: int32 [96, 2], P(('box', 'lev')), may hold values from -2 to 7, as said below
- patch_count: int32 [32], P(('box', 'lev')), may hold values from 1 to 3, as said below
- face_mask: int32 [96, 6], P(('box', 'lev')), may hold values 0 or 1
Outputs:
- updated: float32 [5, 256, 32, 128], P(None, 'box', 'lev')
- ghost: float32 [96, 6, 5, 2048], P(('box', 'lev'))
Inputs may be any that keep to these rules, and one draw needn't show every extreme that they name: `owner_map`: row p is fine patch p of device j = p // 3: column 0 is the offset k of its coarse owner, device (j + k) mod 32, one of -2, -1, 1, 2 and different for the 3 rows of one device; column 1 is a region r of that owner's block, 0 to 7. Rows of patches that are not live carry entries of the same kind and are ignored. No two live patches name the same owner and region. Device j holds live patches j * 3 to j * 3 + patch_count[j] - 1. Some device holds 3 live patches.
All inputs are finite; a program needn't handle non-finite values. No bound on the sum of `face_mask` on one device may be relied on, other than what follows from the above.
Results may differ from a plain program's by a relative error of at most 0.0003.
Values sent between devices are 32-bit elements; how exact they have to be, the bound alone decides.
A program may use at most 128 MiB of HBM per device.

v0:
```python
import functools

import jax
import jax.numpy as jnp
from jax import lax
from jax.experimental import pallas as pl
from jax.experimental.pallas import tpu as pltpu
from jax.sharding import PartitionSpec as P

DELTAS = (-2, -1, 1, 2)
LANES = 128
SUB = 8
F32 = jnp.float32
BF16 = jnp.bfloat16
MESH_ID = pl.DeviceIdType.MESH


def iota(shape, dim):
    return lax.broadcasted_iota(jnp.int32, shape, dim)


def split(values):
    high = values.astype(BF16)
    return high, (values - high.astype(F32)).astype(BF16)


def split_lanes(values):
    return jnp.concatenate(split(values), axis=1)


def times_transposed(left, right):
    return lax.dot_general(left, right, (((1,), (1,)), ((), ())), preferred_element_type=F32)


def both(table):
    return jnp.concatenate([table, table], axis=0)


def window_rows(edge):
    return 14 * edge, 0, 8 * edge, 2 * edge, 12 * edge, 13 * edge


def kernel(
    n_box, n_lev, slots, fields, edge,
    owner, count, fine_far, coarse_far, updated, window,
    fine, coarse, half_a, half_b, send1, recv1, halo_out, halo_in, corner_out, corner_in,
    planes, zrows, send3, recv3, place_table,
    load, s1, r1, s2, r2, s3, r3,
):
    fine_edge = 2 * edge
    block = fields * edge
    ext = edge + SUB
    rows3, z_at, d_at, zd_at, c_at, e_at = window_rows(edge)
    frows = fields * fine_edge
    cut = (fields + 1) // 2
    chunks = ((0, cut), (cut, fields))
    loads = {}
    for part, (f0, f1) in enumerate(chunks):
        for s in range(slots):
            rows = pl.ds(s * frows + f0 * fine_edge, (f1 - f0) * fine_edge)
            loads[part, s] = pltpu.make_async_copy(
                fine_far.at[rows], fine.at[rows], load.at[part * slots + s]
            )
            loads[part, s].start()
    coarse_load = pltpu.make_async_copy(coarse_far, coarse, load.at[2 * slots])
    coarse_load.start()
    n_dev = n_box * n_lev
    box = lax.axis_index("box")
    lev = lax.axis_index("lev")
    me = box * n_lev + lev

    def shifted(by):
        other = lax.rem(me + (by + n_dev), n_dev)
        return (lax.div(other, n_lev), lax.rem(other, n_lev))

    def beside(dx, dy):
        return (lax.rem(box + (dx + n_box), n_box), lax.rem(lev + (dy + n_lev), n_lev))

    sides = (beside(-1, 0), beside(1, 0), beside(0, -1), beside(0, 1))
    corners = tuple(beside(2 * cx - 1, 2 * cy - 1) for cx in (0, 1) for cy in (0, 1))
    barrier = pltpu.get_barrier_semaphore()
    peers = [shifted(delta) for delta in DELTAS] + list(sides) + list(corners)
    for peer in peers:
        pl.semaphore_signal(barrier, inc=1, device_id=peer, device_id_type=MESH_ID)

    live_count = count[0]
    chosen = [
        [(s < live_count) & (owner[0, s] == delta) for delta in DELTAS] for s in range(slots)
    ]
    weight = [[jnp.where(c, 1.0, 0.0).astype(F32) for c in row] for row in chosen]

    q = iota((fine_edge * fine_edge, edge * edge), 0)
    c = iota((fine_edge * fine_edge, edge * edge), 1)
    goal = (q // (2 * fine_edge)) * edge + (q % fine_edge) // 2
    table = jnp.where(goal == c, 0.125, 0.0).astype(BF16)
    for k in range(4):
        region = jnp.int32(-1)
        for s in range(slots):
            region = jnp.where(chosen[s][k], owner[1, s], region)
        send1[k, 0:SUB, :] = jnp.full((SUB, 2 * LANES), 1.0, F32) * region.astype(F32)
    first = []
    for part, (f0, f1) in enumerate(chunks):
        size = (f1 - f0) * edge
        for s in range(slots):
            loads[part, s].wait()
            rows = slice(s * frows + f0 * fine_edge, s * frows + f1 * fine_edge)
            high, low = split(fine[rows, :])
            got = jnp.dot(high, table, preferred_element_type=F32) + jnp.dot(
                low, table, preferred_element_type=F32
            )
            half_a[rows, :] = got[:, :LANES]
            half_b[rows, :] = got[:, LANES:]
        for h, half in enumerate((half_a, half_b)):
            averaged = []
            for s in range(slots):
                at = s * frows + f0 * fine_edge
                averaged.append(
                    half[pl.ds(at, size, stride=2), :] + half[pl.ds(at + 1, size, stride=2), :]
                )
            for k in range(4):
                total = averaged[0] * weight[0][k]
                for s in range(1, slots):
                    total = total + averaged[s] * weight[s][k]
                at = SUB + f0 * edge
                send1[k, at:at + size, h * LANES:(h + 1) * LANES] = total
        if part == 0:
            pl.semaphore_wait(barrier, len(peers))
        start = 0 if part == 0 else SUB + f0 * edge
        rows = pl.ds(start, SUB + f1 * edge - start)
        for k, delta in enumerate(DELTAS):
            copy = pltpu.make_async_remote_copy(
                src_ref=send1.at[k, rows], dst_ref=recv1.at[k, rows],
                send_sem=s1.at[part * 4 + k], recv_sem=r1.at[part * 4 + k],
                device_id=shifted(delta), device_id_type=MESH_ID,
            )
            copy.start()
            first.append(copy)

    for pair in range(4):
        row = iota((LANES, 2 * LANES), 0)
        col = iota((LANES, 2 * LANES), 1)
        hit = (row // edge == 2 * pair + col // LANES) & (row % edge == col % edge)
        place_table[pair] = both(jnp.where(hit, 1.0, 0.0).astype(BF16))
    planes[...] = jnp.zeros_like(planes)
    zrows[...] = jnp.zeros_like(zrows)
    corner_out[...] = jnp.zeros_like(corner_out)
    for k in range(4):
        send3[k * rows3 + e_at:k * rows3 + rows3, :] = jnp.zeros((edge, LANES), F32)
    coarse_load.wait()

    group = (iota((1, LANES), 1) // edge).astype(F32)
    second = []
    for part, (f0, f1) in enumerate(chunks):
        size = (f1 - f0) * edge
        for k in range(4):
            first[part * 4 + k].wait_recv()
        if part == 0:
            region_rows = [recv1[k, 0:1, 0:LANES] for k in range(4)]
            here = [group == region_rows[k] for k in range(4)]
        at = SUB + f0 * edge
        for h in range(2):
            stacked = split_lanes(jnp.concatenate(
                [recv1[k, at:at + size, h * LANES:(h + 1) * LANES] for k in range(4)], axis=0
            ))
            for pair in range(4):
                spread = jnp.dot(stacked, place_table[pair], preferred_element_type=F32)
                for odd in range(2):
                    y = h * SUB + 2 * pair + odd
                    rows = pl.ds(f0 * edge * edge + y, size, stride=edge)
                    merged = coarse[rows, :]
                    for k in range(4):
                        merged = jnp.where(
                            here[k], spread[k * size:(k + 1) * size, odd * LANES:(odd + 1) * LANES], merged
                        )
                    updated[rows, :] = merged
                    if y < 2:
                        halo_out[2, y, f0 * edge:f1 * edge, :] = merged
                    if y >= edge - 2:
                        halo_out[3, edge - 1 - y, f0 * edge:f1 * edge, :] = merged
        for f in range(f0, f1):
            for layer in range(2):
                for side, x in ((0, layer), (1, edge - 1 - layer)):
                    at = f * edge * edge + x * edge
                    halo_out[side, layer, f * edge:(f + 1) * edge, :] = updated[at:at + edge, :]
            for cx in (0, 1):
                for cy in (0, 1):
                    at = f * edge * edge + cx * (edge - 1) * edge + cy * (edge - 1)
                    corner_out[2 * cx + cy, f:f + 1, :] = updated[at:at + 1, :]
        rows = pl.ds(f0 * edge, size)
        for side in (2, 3, 0, 1):
            copy = pltpu.make_async_remote_copy(
                src_ref=halo_out.at[side, :, rows], dst_ref=halo_in.at[side ^ 1, :, rows],
                send_sem=s2.at[part * 4 + side], recv_sem=r2.at[part * 4 + (side ^ 1)],
                device_id=sides[side], device_id_type=MESH_ID,
            )
            copy.start()
            second.append(copy)
    for corner in range(4):
        copy = pltpu.make_async_remote_copy(
            src_ref=corner_out.at[corner], dst_ref=corner_in.at[3 - corner],
            send_sem=s2.at[8 + corner], recv_sem=r2.at[8 + 3 - corner],
            device_id=corners[corner], device_id_type=MESH_ID,
        )
        copy.start()
        second.append(copy)

    lane = iota((1, LANES), 1).astype(F32)

    def pick(k, place):
        t = lane - edge * region_rows[k] - place
        return jnp.where((t == 0.0) | (t == LANES) | (t == -LANES), 1.0, 0.0)

    i_side = iota((ext, 1), 0)
    place = jnp.where(i_side == edge, -1, jnp.where(i_side == edge + 1, edge, i_side)).astype(F32)
    used = i_side < edge + 2
    side_table = jnp.concatenate(
        [jnp.where(used, pick(k, place), 0.0) for k in range(4)], axis=0
    ).astype(BF16)
    side_table = jnp.concatenate([side_table, side_table], axis=1)
    i_z = iota((SUB, 1), 0)
    plus = jnp.where(i_z == 0, -1, jnp.where(i_z == 2, 0, jnp.where(i_z == 1, edge, edge + 1)))
    minus = jnp.where(i_z == 2, -2, edge - 1)
    z_list = []
    for k in range(4):
        up = pick(k, plus.astype(F32))
        down = jnp.where((i_z == 2) | (i_z == 3), pick(k, minus.astype(F32)), 0.0)
        z_list.append(jnp.where(i_z < 4, up - down, 0.0))
    z_table = jnp.concatenate(z_list, axis=0).astype(BF16)
    z_table = jnp.concatenate([z_table, z_table], axis=1)

    def z_store(v, values):
        for k in range(4):
            at = k * rows3
            level = values[k * SUB:k * SUB + 2, :]
            if v < edge:
                send3[pl.ds(at + z_at + v, 2, stride=edge), :] = level
                send3[pl.ds(at + zd_at + v, 2, stride=edge), :] = values[k * SUB + 2:k * SUB + 4, :]
            else:
                send3[pl.ds(at + e_at + 8 + v - edge, 2, stride=2), :] = level

    for v in range(edge):
        for f in range(fields):
            zrows[pl.ds(v * LANES + f, edge, stride=SUB), :] = updated[
                pl.ds(f * edge * edge + v, edge, stride=edge), :
            ]
    for v in range(0, edge, 2):
        got = times_transposed(z_table, split_lanes(zrows[v * LANES:(v + 2) * LANES, :]))
        z_store(v, got[:, :LANES])
        z_store(v + 1, got[:, LANES:])

    third = []

    def send_back(part):
        start, size = ((0, 4 * edge), (4 * edge, rows3 - 4 * edge))[part]
        for k, delta in enumerate(DELTAS):
            copy = pltpu.make_async_remote_copy(
                src_ref=send3.at[pl.ds(k * rows3 + start, size)], dst_ref=recv3.at[k, pl.ds(start, size)],
                send_sem=s3.at[part * 4 + k], recv_sem=r3.at[part * 4 + k],
                device_id=shifted(-delta), device_id_type=MESH_ID,
            )
            copy.start()
            third.append(copy)

    send_back(0)
    for copy in second:
        copy.wait_recv()

    for side in range(4):
        near = 1.0 if side % 2 == 0 else -1.0
        for f in range(fields):
            a = f * edge
            adjacent = halo_in[side, 0, a:a + edge, :]
            far = halo_in[side, 1, a:a + edge, :]
            own = halo_out[side, 0, a:a + edge, :]
            planes[pl.ds(2 * side * LANES + f, edge, stride=SUB), :] = adjacent
            planes[pl.ds((2 * side + 1) * LANES + f, edge, stride=SUB), :] = (own - far) * near
    for corner in range(4):
        planes[8 * LANES + corner * SUB:8 * LANES + (corner + 1) * SUB, :] = corner_in[corner]
    for side in range(4):
        both_planes = split_lanes(planes[2 * side * LANES:(2 * side + 2) * LANES, :])
        got = times_transposed(side_table, both_planes)
        for k in range(4):
            at = k * rows3
            send3[at + (4 + side) * edge:at + (5 + side) * edge, :] = got[k * ext:k * ext + edge, :LANES]
            send3[at + e_at + 2 * side:at + e_at + 2 * side + 2, :] = (
                got[k * ext + edge:k * ext + edge + 2, :LANES]
            )
            to = at + d_at + side * edge
            send3[to:to + edge, :] = got[k * ext:k * ext + edge, LANES:]
        if side >= 2:
            z_store(edge + side - 2, times_transposed(z_table, both_planes[:LANES, :]))
    got = times_transposed(side_table, split_lanes(planes[8 * LANES:9 * LANES, :]))
    for k in range(4):
        send3[k * rows3 + c_at:k * rows3 + c_at + edge, :] = got[k * ext:k * ext + edge, :]

    send_back(1)
    for copy in third:
        copy.wait_recv()

    for s in range(slots):
        total = recv3[0] * weight[s][0]
        for k in range(1, 4):
            total = total + recv3[k] * weight[s][k]
        window[s] = total

    for copy in first + second + third:
        copy.wait_send()


def ghost_kernel(
    slots, fields, edge, count, mask, window, updated_in, updated_out, ghost_out,
    passing, ghost, pass_sem, out_sem,
):
    fine_edge = 2 * edge
    rows3, z_at, d_at, zd_at, c_at, e_at = window_rows(edge)
    live_count = count[0]
    into = pltpu.make_async_copy(updated_in, passing, pass_sem.at[0])
    into.start()

    def line_tables(cell, odd, pair):
        i = iota((2 * edge, LANES), 0)
        at = jnp.where(i == edge + pair, -1, jnp.where(i == edge + pair + 1, edge, i))
        at = jnp.where((i < edge) | (at != i), at, -9)
        plain = jnp.where(at == cell, 1.0, 0.0)
        sign = jnp.where(odd, 0.125, -0.125)
        slope = jnp.where(at == cell + 1, sign, jnp.where(at == cell - 1, -sign, 0.0))
        full = both(jnp.concatenate([plain, plain + slope], axis=1)).astype(BF16)
        return full, both((plain[:edge] * 0.125)).astype(BF16)

    l2 = iota((2 * edge, LANES), 1)
    side_tables = []
    for side in range(4):
        full, w_diff = line_tables((l2 % fine_edge) // 2, l2 % 2 == 1, 2 * side)
        side_tables.append(full)
    z_tables = []
    for z in range(2):
        full, v_diff = line_tables(
            (l2 % (2 * fine_edge)) // 4, (l2 // 2) % 2 == 1, 8 + 2 * z
        )
        z_tables.append(full)
    row = iota((LANES, LANES), 0)
    col = iota((LANES, LANES), 1)
    line_v = both(jnp.where(row // SUB == (col % (2 * fine_edge)) // 4, 1.0, 0.0).astype(BF16))

    lanes8 = iota((SUB, LANES), 1)
    low_half = lanes8 < 2 * fine_edge
    half_sign = jnp.where(low_half, -0.125, 0.125)
    quarter = (lanes8 // fine_edge) % 2 == 1
    quarter_slope = jnp.where(quarter, 0.125, -0.125)
    quarter_sign = jnp.where(quarter, 1.0, -1.0)
    last_sign = jnp.where(lanes8 % 2 == 1, 1.0, -1.0)
    own_field = lanes8 % SUB == iota((SUB, LANES), 0)

    def spread_plane(s, at, table, ends=None):
        total = window[s, at:at + edge, :]
        if ends is not None:
            total = jnp.concatenate([total, ends], axis=0)
        high = total.astype(BF16).astype(F32)
        tall = jnp.concatenate([high, total - high], axis=0)
        return jnp.dot(tall.T.astype(BF16), table, preferred_element_type=F32)

    def cut(values, m):
        return values[m * SUB:(m + 1) * SUB, :]

    outs = []
    for s in range(slots):
        keep = [
            jnp.where((s < live_count) & (mask[s, face] > 0), 1.0, 0.0).astype(F32)
            for face in range(6)
        ]
        ends_all = window[s, e_at:e_at + edge, :]
        lines = spread_plane(s, c_at, w_diff)
        line = [cut(lines, corner) * 8.0 for corner in range(4)]
        edges = []
        for side in range(4):
            centre = spread_plane(s, (4 + side) * edge, side_tables[side], ends_all)
            diff = spread_plane(s, d_at + side * edge, w_diff)
            plain = [cut(centre, m)[:, :LANES] for m in range(edge)]
            full = [cut(centre, m)[:, LANES:] for m in range(edge)]
            high_side = side % 2
            if side < 2:
                edges.append(ends_all[2 * side:2 * side + 1, :])
                edges.append(ends_all[2 * side + 1:2 * side + 2, :])
                around = [line[2 * high_side]] + plain + [line[2 * high_side + 1]]
                for t in range(edge // 2):
                    base = jnp.where(low_half, full[2 * t], full[2 * t + 1])
                    slope = jnp.where(
                        low_half, around[2 * t + 2] - around[2 * t], around[2 * t + 3] - around[2 * t + 1]
                    )
                    across = jnp.where(low_half, cut(diff, 2 * t), cut(diff, 2 * t + 1))
                    base = base + slope * quarter_slope
                    at = t * LANES
                    ghost[s, :, side, at:at + LANES] = ((base - across) * keep[side])[:fields]
                    at = at + fine_edge * fine_edge
                    ghost[s, :, side, at:at + LANES] = ((base + across) * keep[side])[:fields]
            else:
                around = [line[high_side]] + plain + [line[2 + high_side]]
                for t in range(edge):
                    value = (
                        full[t] + (around[t + 2] - around[t]) * half_sign + cut(diff, t) * quarter_sign
                    )
                    ghost[s, :, side, t * LANES:(t + 1) * LANES] = (value * keep[side])[:fields]
        tall = jnp.concatenate([jnp.where(own_field, e, 0.0) for e in edges], axis=0)
        ends = jnp.dot(split_lanes(tall), line_v, preferred_element_type=F32)
        for z in range(2):
            centre = spread_plane(s, z_at + z * edge, z_tables[z], ends_all)
            diff = spread_plane(s, zd_at + z * edge, v_diff)
            around = (
                [cut(ends, z)] + [cut(centre, m)[:, :LANES] for m in range(edge)] + [cut(ends, 2 + z)]
            )
            for t in range(edge):
                value = (
                    cut(centre, t)[:, LANES:]
                    + (around[t + 2] - around[t]) * half_sign
                    + cut(diff, t) * last_sign
                )
                ghost[s, :, 4 + z, t * LANES:(t + 1) * LANES] = (value * keep[4 + z])[:fields]
        outs.append(pltpu.make_async_copy(ghost.at[s], ghost_out.at[s], out_sem.at[s]))
        outs[-1].start()
        if s == 0:
            into.wait()
            outs.append(pltpu.make_async_copy(passing, updated_out, pass_sem.at[1]))
            outs[-1].start()
    for copy in outs:
        copy.wait()


def body(n_box, n_lev, fine, coarse, owner_map, patch_count, face_mask):
    slots, fields, fine_edge, _ = fine.shape
    edge = fine_edge // 2
    block = fields * edge
    rows3 = window_rows(edge)[0]
    vmem = pl.BlockSpec(memory_space=pltpu.VMEM)
    smem = pl.BlockSpec(memory_space=pltpu.SMEM)
    far = pl.BlockSpec(memory_space=pl.ANY)
    flat = jax.ShapeDtypeStruct((block * edge, LANES), F32)
    updated, window = pl.pallas_call(
        functools.partial(kernel, n_box, n_lev, slots, fields, edge),
        out_shape=(flat, jax.ShapeDtypeStruct((slots, rows3, LANES), F32)),
        in_specs=[smem, smem, far, far],
        out_specs=(vmem, vmem),
        scratch_shapes=[
            pltpu.VMEM((slots * fields * fine_edge, fine_edge * fine_edge), F32),
            pltpu.VMEM((block * edge, LANES), F32),
            pltpu.VMEM((slots * fields * fine_edge, LANES), F32),
            pltpu.VMEM((slots * fields * fine_edge, LANES), F32),
            pltpu.VMEM((4, block + SUB, 2 * LANES), F32),
            pltpu.VMEM((4, block + SUB, 2 * LANES), F32),
            pltpu.VMEM((4, 2, block, LANES), F32),
            pltpu.VMEM((4, 2, block, LANES), F32),
            pltpu.VMEM((4, SUB, LANES), F32),
            pltpu.VMEM((4, SUB, LANES), F32),
            pltpu.VMEM((9 * LANES, LANES), F32),
            pltpu.VMEM((edge * LANES, LANES), F32),
            pltpu.VMEM((4 * rows3, LANES), F32),
            pltpu.VMEM((4, rows3, LANES), F32),
            pltpu.VMEM((4, 2 * LANES, 2 * LANES), BF16),
            pltpu.SemaphoreType.DMA((2 * slots + 1,)),
            pltpu.SemaphoreType.DMA((8,)),
            pltpu.SemaphoreType.DMA((8,)),
            pltpu.SemaphoreType.DMA((12,)),
            pltpu.SemaphoreType.DMA((12,)),
            pltpu.SemaphoreType.DMA((8,)),
            pltpu.SemaphoreType.DMA((8,)),
        ],
        compiler_params=pltpu.CompilerParams(collective_id=0, has_side_effects=True),
    )(
        owner_map.T, patch_count,
        fine.reshape(slots * fields * fine_edge, fine_edge * fine_edge),
        coarse.reshape(block * edge, LANES),
    )
    ghost_shape = (slots, fields, 6, 2 * fine_edge * fine_edge)
    updated, ghost = pl.pallas_call(
        functools.partial(ghost_kernel, slots, fields, edge),
        out_shape=(flat, jax.ShapeDtypeStruct(ghost_shape, F32)),
        in_specs=[smem, smem, vmem, far],
        out_specs=(far, far),
        scratch_shapes=[
            pltpu.VMEM((block * edge, LANES), F32),
            pltpu.VMEM(ghost_shape, F32),
            pltpu.SemaphoreType.DMA((2,)),
            pltpu.SemaphoreType.DMA((slots,)),
        ],
    )(patch_count, face_mask, window, updated)
    return updated.reshape(coarse.shape), ghost.transpose(0, 2, 1, 3)


def solution(mesh):
    return jax.shard_map(
        functools.partial(body, mesh.shape["box"], mesh.shape["lev"]),
        mesh=mesh,
        in_specs=(
            P(("box", "lev"), None, None, None),
            P(None, "box", "lev", None),
            P(("box", "lev"), None),
            P(("box", "lev")),
            P(("box", "lev"), None),
        ),
        out_specs=(P(None, "box", "lev", None), P(("box", "lev"), None, None, None)),
        check_vma=False,
    )
```

profile of v0, /device:TPU:0, one launch (start us, length us, event | category | flops | bytes accessed | tf_op | source)
XLA Modules:
  0.0 31.0 jit_solution(16410067914183349750)
XLA Ops:
  1.3 26.2 %shard_map.68 = (f32[1280,128]{1,0:T(8,128)}, f32[3,224,128]{2,1,0:T(8,128)}) custom-call(s32[2,3]{1,0:T(2,128)} %bitcast.7, s32[1]{0:T(128)S(6)} %copy.7.count, f32[480,1024]{1,0:T(8,128)} %bitcast.5, f32[1280,128]{1,0:T(8,128)} %bitcast.6), custom_call_target="tpu_custom_call" | custom-call | tf_op jit(solution)/shard_map/pallas_call | solution.py:437
  27.5 3.6 %shard_map.69 = (f32[1280,128]{1,0:T(8,128)}, f32[3,5,6,2048]{3,2,1,0:T(8,128)}) custom-call(s32[1]{0:T(128)S(6)} %copy.7.count, s32[3,6]{1,0:T(4,128)} %mask.1, f32[3,224,128]{2,1,0:T(8,128)} %get-tuple-element.6.window, f32[1280,128]{1,0:T(8,128)} %get-tuple-element.7.updated_in), custom_call_target="tpu_custom_call" | custom-call | tf_op jit(solution)/shard_map/pallas_call | solution.py:473
where the time goes:
time: 31.3 us; the launch traced here: 31 us
  Pallas kernels  29.8 us (95%)
  between operations  1.29 us (4%)
    pallas_call x1, Pallas kernels, body(): pl.pallas_call(functools.partial(kernel, n_box, n_lev, slots, fields, edg...  26.2 us
    pallas_call x1, Pallas kernels, body(): pl.pallas_call(functools.partial(ghost_kernel, slots, fields, edge), out_...  3.59 us

commit v1 on v0

--- a/solution.py
+++ b/solution.py
@@ -309,13 +309,13 @@
 
 def ghost_kernel(
     slots, fields, edge, count, mask, window, updated_in, updated_out, ghost_out,
-    passing, ghost, pass_sem, out_sem,
+    ghost, pass_sem, out_sem,
 ):
     fine_edge = 2 * edge
     rows3, z_at, d_at, zd_at, c_at, e_at = window_rows(edge)
     live_count = count[0]
-    into = pltpu.make_async_copy(updated_in, passing, pass_sem.at[0])
-    into.start()
+    outs = [pltpu.make_async_copy(updated_in, updated_out, pass_sem.at[0])]
+    outs[0].start()
 
     def line_tables(cell, odd, pair):
         i = iota((2 * edge, LANES), 0)
@@ -362,7 +362,6 @@
     def cut(values, m):
         return values[m * SUB:(m + 1) * SUB, :]
 
-    outs = []
     for s in range(slots):
         keep = [
             jnp.where((s < live_count) & (mask[s, face] > 0), 1.0, 0.0).astype(F32)
@@ -417,10 +416,6 @@
                 ghost[s, :, 4 + z, t * LANES:(t + 1) * LANES] = (value * keep[4 + z])[:fields]
         outs.append(pltpu.make_async_copy(ghost.at[s], ghost_out.at[s], out_sem.at[s]))
         outs[-1].start()
-        if s == 0:
-            into.wait()
-            outs.append(pltpu.make_async_copy(passing, updated_out, pass_sem.at[1]))
-            outs[-1].start()
     for copy in outs:
         copy.wait()
 
@@ -432,12 +427,12 @@
     rows3 = window_rows(edge)[0]
     vmem = pl.BlockSpec(memory_space=pltpu.VMEM)
     smem = pl.BlockSpec(memory_space=pltpu.SMEM)
-    far = pl.BlockSpec(memory_space=pl.ANY)
+    hbm = pl.BlockSpec(memory_space=pltpu.HBM)
     flat = jax.ShapeDtypeStruct((block * edge, LANES), F32)
     updated, window = pl.pallas_call(
         functools.partial(kernel, n_box, n_lev, slots, fields, edge),
         out_shape=(flat, jax.ShapeDtypeStruct((slots, rows3, LANES), F32)),
-        in_specs=[smem, smem, far, far],
+        in_specs=[smem, smem, hbm, hbm],
         out_specs=(vmem, vmem),
         scratch_shapes=[
             pltpu.VMEM((slots * fields * fine_edge, fine_edge * fine_edge), F32),
@@ -463,7 +458,7 @@
             pltpu.SemaphoreType.DMA((8,)),
             pltpu.SemaphoreType.DMA((8,)),
         ],
-        compiler_params=pltpu.CompilerParams(collective_id=0, has_side_effects=True),
+        compiler_params=pltpu.CompilerParams(collective_id=0, has_side_effects=True, vmem_limit_bytes=55000000),
     )(
         owner_map.T, patch_count,
         fine.reshape(slots * fields * fine_edge, fine_edge * fine_edge),
@@ -473,14 +468,14 @@
     updated, ghost = pl.pallas_call(
         functools.partial(ghost_kernel, slots, fields, edge),
         out_shape=(flat, jax.ShapeDtypeStruct(ghost_shape, F32)),
-        in_specs=[smem, smem, vmem, far],
-        out_specs=(far, far),
+        in_specs=[smem, smem, vmem, vmem],
+        out_specs=(hbm, hbm),
         scratch_shapes=[
-            pltpu.VMEM((block * edge, LANES), F32),
             pltpu.VMEM(ghost_shape, F32),
-            pltpu.SemaphoreType.DMA((2,)),
+            pltpu.SemaphoreType.DMA((1,)),
             pltpu.SemaphoreType.DMA((slots,)),
         ],
+        compiler_params=pltpu.CompilerParams(vmem_limit_bytes=16777216),
     )(patch_count, face_mask, window, updated)
     return updated.reshape(coarse.shape), ghost.transpose(0, 2, 1, 3)
 

time: 31.3 us -> 29.6 us (0.946)
  Pallas kernels: 29.8 us -> 27.5 us
  local copies, waits for them, and re-layouts: 0 us -> 0.68 us
    pallas_call x1, Pallas kernels: 3.59 us -> 2.42 us  [body(): pl.pallas_call(functools.partial(ghost_kernel, slots, fields, edge), out_...]
    pallas_call x1, Pallas kernels: 26.2 us -> 25 us  [body(): pl.pallas_call(functools.partial(kernel, n_box, n_lev, slots, fields, edg...]
    unnamed x0 -> x4, local copies, waits for them, and re-layouts: none -> 0.68 us
where the time goes in v1:
time: 29.6 us; the launch traced here: 29.5 us
  Pallas kernels  27.5 us (93%)
  between operations  1.32 us (4%)
  local copies, waits for them, and re-layouts  0.68 us (2%)
    pallas_call x1, Pallas kernels, body(): pl.pallas_call(functools.partial(kernel, n_box, n_lev, slots, fields, edg...  25 us
    pallas_call x1, Pallas kernels, body(): pl.pallas_call(functools.partial(ghost_kernel, slots, fields, edge), out_...  2.42 us
    unnamed x4, local copies, waits for them, and re-layouts  0.68 us

profile of v1, /device:TPU:0, one launch (start us, length us, event | category | flops | bytes accessed | tf_op | source)
XLA Modules:
  0.0 29.5 jit_solution(15109667524310407750)
XLA Ops:
  0.6 0.0 copy-start
  1.3 0.0 copy-start.1
  1.3 0.7 %copy-done.1 = s32[3,2]{0,1:T(2,128)S(1)} copy-done((s32[3,2]{0,1:T(2,128)S(1)}, s32[3,2]{0,1:T(2,128)}, u32[]{:S(2)}) %copy-start.1) | copy-done | bytes 48
  2.0 25.0 %shard_map.68 = (f32[1280,128]{1,0:T(8,128)S(1)}, f32[3,224,128]{2,1,0:T(8,128)S(1)}) custom-call(s32[2,3]{1,0:T(2,128)S(1)} %bitcast.5, s32[1]{0:T(128)S(6)} %copy.7.count, f32[480,1024]{1,0:T(8,128)} %bitcast.6, f32[1280,128]{1,0:T(8,128)} %bitcast.7), custom_call_target="tpu_custom_call" | custom-call | tf_op jit(solution)/shard_map/pallas_call | solution.py:432
  27.0 0.0 copy-done
  27.0 2.4 %shard_map.69 = (f32[1280,128]{1,0:T(8,128)}, f32[3,5,6,2048]{3,2,1,0:T(8,128)}) custom-call(s32[1]{0:T(128)S(6)} %copy.7.count, s32[3,6]{1,0:T(4,128)S(1)} %copy-done, f32[3,224,128]{2,1,0:T(8,128)S(1)} %get-tuple-element.6.window, f32[1280,128]{1,0:T(8,128)S(1)} %get-tuple-element.7.updated_in), custom_call_target="tpu_custom_call" | custom-call | tf_op jit(solution)/shard_map/pallas_call | solution.py:468
Async XLA Ops:
  0.6 26.4 %copy-start = (s32[3,6]{1,0:T(4,128)S(1)}, s32[3,6]{1,0:T(4,128)}, u32[]{:S(2)}) copy-start(s32[3,6]{1,0:T(4,128)} %mask.1) | copy-start | bytes 220
  1.3 0.7 %copy-start.1 = (s32[3,2]{0,1:T(2,128)S(1)}, s32[3,2]{0,1:T(2,128)}, u32[]{:S(2)}) copy-start(s32[3,2]{0,1:T(2,128)} %param.7) | copy-start | bytes 76

commit v2 on v1

v2 whole, which is shorter than its diff:
```python
import functools

import jax
import jax.numpy as jnp
from jax import lax
from jax.experimental import pallas as pl
from jax.experimental.pallas import tpu as pltpu
from jax.sharding import PartitionSpec as P

DELTAS = (-2, -1, 1, 2)
LANES = 128
SUB = 8
F32 = jnp.float32
BF16 = jnp.bfloat16
MESH_ID = pl.DeviceIdType.MESH


def iota(shape, dim):
    return lax.broadcasted_iota(jnp.int32, shape, dim)


def split(values):
    high = values.astype(BF16)
    return high, (values - high.astype(F32)).astype(BF16)


def split_lanes(values):
    return jnp.concatenate(split(values), axis=1)


def times_transposed(left, right):
    return lax.dot_general(left, right, (((1,), (1,)), ((), ())), preferred_element_type=F32)


def both(table):
    return jnp.concatenate([table, table], axis=0)


def transposed_groups(arrays, edge):
    out = list(arrays)
    group = iota(out[0].shape, 1) // edge
    for bit in (4, 2, 1):
        low = (group // bit) % 2 == 0
        for i in range(8):
            if i & bit == 0:
                a, b = out[i], out[i + bit]
                out[i] = jnp.where(low, a, pltpu.roll(b, bit * edge, 1))
                out[i + bit] = jnp.where(low, pltpu.roll(a, LANES - bit * edge, 1), b)
    return out


class Layout:
    def __init__(self, fields, edge):
        self.ends = 4 * fields
        self.side = 4 * fields + 4
        self.z = 4 * self.side
        self.corner = self.z + 8 * fields
        self.own = self.corner + 8
        self.rows = self.own + 12 * fields + 8
        self.rows = self.rows + (-self.rows) % SUB


DIRECTIONS = ((-1, 0), (1, 0), (0, -1), (0, 1), (-1, -1), (-1, 1), (1, -1), (1, 1))


def opposite(d):
    return d ^ 1 if d < 4 else 11 - d


def relations(n_box, n_lev):
    n_dev = n_box * n_lev
    offsets, same = set(), {}
    for me in range(n_dev):
        box, lev = divmod(me, n_lev)

        def add(other):
            db, dl = (other // n_lev - box) % n_box, (other % n_lev - lev) % n_lev
            offsets.add((db, dl))
            offsets.add((-db % n_box, -dl % n_lev))

        for delta in DELTAS:
            add((me + delta) % n_dev)
        for d, (dx, dy) in enumerate(DIRECTIONS):
            owner = ((box - dx) % n_box) * n_lev + (lev - dy) % n_lev
            add(owner)
            for k, delta in enumerate(DELTAS):
                target = (owner - delta) % n_dev
                add(target)
                same.setdefault((d, k), set()).add(target == me)
    offsets.discard((0, 0))
    return sorted(offsets), same


def kernel(
    n_box, n_lev, slots, fields, edge,
    owner, count, fine_far, coarse_far, updated, window,
    fine, coarse, half_a, half_b, avg, own_got, send1, recv1, region_out, region_in, near_in,
    upd, corner_lines, corner_region, side_out, side_in, z_out, z_in, corner_out, corner_in,
    place_table,
    load, s1, r1, sh, rh, s3, r3,
):
    fine_edge = 2 * edge
    block = fields * edge
    plane = edge * edge
    lay = Layout(fields, edge)
    frows = fields * fine_edge
    cut = (fields + 1) // 2
    chunks = ((0, cut), (cut, fields))
    loads = {}
    for part, (f0, f1) in enumerate(chunks):
        for s in range(slots):
            rows = pl.ds(s * frows + f0 * fine_edge, (f1 - f0) * fine_edge)
            loads[part, s] = pltpu.make_async_copy(
                fine_far.at[rows], fine.at[rows], load.at[part * slots + s]
            )
            loads[part, s].start()
    coarse_load = pltpu.make_async_copy(coarse_far, coarse, load.at[2 * slots])
    coarse_load.start()
    n_dev = n_box * n_lev
    offsets, same = relations(n_box, n_lev)
    box = lax.axis_index("box")
    lev = lax.axis_index("lev")
    me = box * n_lev + lev

    def at(linear):
        return (lax.div(linear, n_lev), lax.rem(linear, n_lev))

    def shifted(by):
        return at(lax.rem(me + (by + n_dev), n_dev))

    def beside(dx, dy):
        return (lax.rem(box + (dx + n_box), n_box), lax.rem(lev + (dy + n_lev), n_lev))

    around = [beside(dx, dy) for dx, dy in DIRECTIONS]
    barrier = pltpu.get_barrier_semaphore()
    for db, dl in offsets:
        pl.semaphore_signal(barrier, inc=1, device_id=beside(db, dl), device_id_type=MESH_ID)

    live_count = count[0]
    chosen = [
        [(s < live_count) & (owner[0, s] == delta) for delta in DELTAS] for s in range(slots)
    ]
    weight = [[jnp.where(c, 1.0, 0.0).astype(F32) for c in row] for row in chosen]
    for k in range(4):
        region = jnp.int32(-1)
        for s in range(slots):
            region = jnp.where(chosen[s][k], owner[1, s], region)
        region_out[k] = jnp.full((1, LANES), 1.0, F32) * region.astype(F32)

    q = iota((fine_edge * fine_edge, plane), 0)
    c = iota((fine_edge * fine_edge, plane), 1)
    goal = (q // (2 * fine_edge)) * edge + (q % fine_edge) // 2
    table = jnp.where(goal == c, 0.125, 0.0).astype(BF16)
    first, told = [], []
    order = (1, 2, 0, 3)
    for part, (f0, f1) in enumerate(chunks):
        size = (f1 - f0) * edge
        for s in range(slots):
            loads[part, s].wait()
            rows = slice(s * frows + f0 * fine_edge, s * frows + f1 * fine_edge)
            high, low = split(fine[rows, :])
            got = jnp.dot(high, table, preferred_element_type=F32) + jnp.dot(
                low, table, preferred_element_type=F32
            )
            half_a[rows, :] = got[:, :LANES]
            half_b[rows, :] = got[:, LANES:]
        to = f0 * edge
        for h, half in enumerate((half_a, half_b)):
            averaged = []
            for s in range(slots):
                start = s * frows + f0 * fine_edge
                mean = half[pl.ds(start, size, stride=2), :] + half[pl.ds(start + 1, size, stride=2), :]
                start = (h * slots + s) * block + to
                avg[start:start + size, :] = mean
                averaged.append(mean)
            for k in range(4):
                total = averaged[0] * weight[0][k]
                for s in range(1, slots):
                    total = total + averaged[s] * weight[s][k]
                send1[k, to:to + size, h * LANES:(h + 1) * LANES] = total
        if part == 0:
            pl.semaphore_wait(barrier, len(offsets))
            for k in order:
                copy = pltpu.make_async_remote_copy(
                    src_ref=region_out.at[k], dst_ref=region_in.at[k],
                    send_sem=sh.at[k], recv_sem=rh.at[k],
                    device_id=shifted(DELTAS[k]), device_id_type=MESH_ID,
                )
                copy.start()
                told.append(copy)
        for k in order:
            copy = pltpu.make_async_remote_copy(
                src_ref=send1.at[k, pl.ds(to, size)], dst_ref=recv1.at[k, pl.ds(to, size)],
                send_sem=s1.at[part * 4 + k], recv_sem=r1.at[part * 4 + k],
                device_id=shifted(DELTAS[k]), device_id_type=MESH_ID,
            )
            copy.start()
            first.append(copy)

    for copy in told:
        copy.wait_recv()
    passed = []
    for d in range(8):
        copy = pltpu.make_async_remote_copy(
            src_ref=region_in, dst_ref=near_in.at[opposite(d)],
            send_sem=sh.at[4 + d], recv_sem=rh.at[4 + opposite(d)],
            device_id=around[d], device_id_type=MESH_ID,
        )
        copy.start()
        passed.append(copy)

    for pair in range(4):
        row = iota((LANES, 2 * LANES), 0)
        col = iota((LANES, 2 * LANES), 1)
        hit = (row // edge == 2 * pair + col // LANES) & (row % edge == col % edge)
        place_table[pair] = both(jnp.where(hit, 1.0, 0.0).astype(BF16))

    row = iota((plane, 4 * LANES), 0)
    col = iota((plane, 4 * LANES), 1)
    kind = col // LANES
    inner = col % edge
    fixed = jnp.where(kind % 2 == 0, 0, edge - 1)
    hit = jnp.where(kind < 2, fixed * edge + inner, inner * edge + fixed) == row
    own_table = jnp.where(hit, 1.0, 0.0).astype(BF16)
    high, low = split(jnp.concatenate(
        [avg[:slots * block, :], avg[slots * block:, :]], axis=1
    ))
    got = jnp.dot(high, own_table, preferred_element_type=F32) + jnp.dot(
        low, own_table, preferred_element_type=F32
    )
    for kind in range(4):
        own_got[kind * slots * block:(kind + 1) * slots * block, :] = got[
            :, kind * LANES:(kind + 1) * LANES
        ]
    group_f = iota((fields, LANES), 1) // edge
    for s in range(slots):
        for h in range(2):
            for side in range(2):
                start = (h * slots + s) * block + side * (edge - 1)
                to = lay.own + (2 * side + h) * fields
                window[s, to:to + fields, :] = avg[pl.ds(start, fields, stride=edge), :]
            for kind in range(4):
                total = jnp.zeros((fields, LANES), F32)
                for i in range(8):
                    start = (kind * slots + s) * block + h * 8 + i
                    part = own_got[pl.ds(start, fields, stride=edge), :]
                    total = jnp.where(group_f == i, part, total)
                to = lay.own + (2 * (2 + kind) + h) * fields
                window[s, to:to + fields, :] = total

    corner_lines[...] = jnp.zeros_like(corner_lines)
    coarse_load.wait()
    for copy in passed:
        copy.wait_recv()

    lane = iota((1, LANES), 1).astype(F32)
    here_rows = [region_in[k] for k in range(4)]

    def pick(region, place):
        t = lane - edge * region - place
        return jnp.where((t == 0.0) | (t == LANES) | (t == -LANES), 1.0, 0.0)

    z_rows = []
    for depth in range(2):
        for k in range(4):
            for place in (-1 - depth, edge + depth):
                z_rows.append(pick(here_rows[k], place))
    for d in (1, 0):
        for place in (-1, edge):
            for k in range(4):
                z_rows.append(pick(near_in[d, k], place))
    z_table = jnp.concatenate(z_rows, axis=0).astype(BF16)
    z_table = jnp.concatenate([z_table, z_table], axis=1)
    for corner in range(4):
        for k in range(4):
            corner_region[k, corner:corner + 1, :] = near_in[opposite(4 + corner), k]

    group = (iota((1, LANES), 1) // edge).astype(F32)
    here = [group == region for region in here_rows]
    group8 = iota((SUB, LANES), 1) // edge
    end_lines = [jnp.zeros((SUB, LANES), F32) for _ in range(2)]
    for part, (f0, f1) in enumerate(chunks):
        size = (f1 - f0) * edge
        for k in range(4):
            first[part * 4 + k].wait_recv()
        to = f0 * edge
        for h in range(2):
            stacked = split_lanes(jnp.concatenate(
                [recv1[k, to:to + size, h * LANES:(h + 1) * LANES] for k in range(4)], axis=0
            ))
            for pair in range(4):
                spread = jnp.dot(stacked, place_table[pair], preferred_element_type=F32)
                for odd in range(2):
                    y = h * SUB + 2 * pair + odd
                    rows = pl.ds(f0 * plane + y, size, stride=edge)
                    merged = coarse[rows, :]
                    for k in range(4):
                        merged = jnp.where(
                            here[k], spread[k * size:(k + 1) * size, odd * LANES:(odd + 1) * LANES], merged
                        )
                    upd[rows, :] = merged
                    updated[rows, :] = merged
        for f in range(f0, f1):
            got = times_transposed(z_table, split_lanes(upd[f * plane:(f + 1) * plane, :]))
            for depth in range(2):
                for h in range(2):
                    z_out[pl.ds((2 * depth + h) * fields + f, 8, stride=4 * fields), :] = got[
                        depth * 8:(depth + 1) * 8, h * LANES:(h + 1) * LANES
                    ]
            high_end = got[16:24, LANES:]
            if f:
                high_end = pltpu.roll(high_end, LANES - f * edge, 1)
            low_end = pltpu.roll(got[24:32, :LANES], LANES - (f + 1) * edge, 1)
            end_lines[0] = jnp.where(group8 == 7 - f, high_end, end_lines[0])
            end_lines[1] = jnp.where(group8 == 7 - f, low_end, end_lines[1])

    third = []

    def send(src, dst, slot, d, k, target):
        kinds = {False} if d is None else same[d, k]
        remote = local = itself = None
        if False in kinds:
            remote = pltpu.make_async_remote_copy(
                src_ref=src, dst_ref=dst, send_sem=s3.at[slot], recv_sem=r3.at[slot],
                device_id=target, device_id_type=MESH_ID,
            )
        if True in kinds:
            local = pltpu.make_async_copy(src, dst, r3.at[slot])
        if local is None:
            remote.start()
        elif remote is None:
            local.start()
        else:
            itself = (target[0] == box) & (target[1] == lev)
            pl.when(itself)(local.start)
            pl.when(jnp.logical_not(itself))(remote.start)
        third.append((remote, local, itself))

    def target_of(d, k):
        other = around[opposite(d)]
        linear = other[0] * n_lev + other[1]
        return at(lax.rem(linear + (n_dev - DELTAS[k]), n_dev))

    z_size = 8 * fields
    for k in order:
        send(z_out.at[pl.ds(k * z_size, z_size)], z_in.at[k], k, None, k, shifted(-DELTAS[k]))

    field_step = plane
    sublane = iota((SUB, LANES), 0)
    in_group = iota((SUB, LANES), 1) % edge
    for d in (0, 1, 2, 3):
        outer, inner = (edge, 1) if d < 2 else (1, edge)
        adjacent = edge - 1 if d % 2 == 0 else 0
        far = edge - 2 if d % 2 == 0 else 1
        lines = []
        for i in range(8):
            lines.append(jnp.concatenate([
                upd[pl.ds(level * outer + (h * 8 + i) * inner, SUB, stride=field_step), :]
                for level in (adjacent, far) for h in range(2)
            ], axis=0))
        by_region = transposed_groups(lines, edge)
        ends = []
        for g in range(8):
            before = by_region[(g + 7) % 8][:2 * SUB]
            after = by_region[(g + 1) % 8][:2 * SUB]
            ends.append(jnp.where(iota((2 * SUB, LANES), 1) % edge == 0, after, before))
        for k in range(4):
            region = near_in[opposite(d), k]
            total = by_region[0]
            end = ends[0]
            for g in range(1, 8):
                hit = region == float(g)
                total = jnp.where(hit, by_region[g], total)
                end = jnp.where(hit, ends[g], end)
            base = (d * 4 + k) * lay.side
            for part in range(4):
                side_out[base + part * fields:base + (part + 1) * fields, :] = total[
                    part * SUB:part * SUB + fields, :
                ]
            for h in range(2):
                used = (sublane < fields) & ((in_group == 0) | (in_group == edge - 1))
                one = jnp.where(used, end[h * SUB:(h + 1) * SUB, :], 0.0)
                for bit in (1, 2, 4):
                    moved = pltpu.roll(one, LANES - 2 * bit, 1)
                    one = jnp.where((sublane // bit) % 2 == 1, moved, one)
                side_out[base + lay.ends + h:base + lay.ends + h + 1, :] = jnp.sum(
                    one, axis=0, keepdims=True
                )
        if d < 2:
            for e in range(2):
                side_out[pl.ds(d * 4 * lay.side + lay.ends + 2 + e, 4, stride=lay.side), :] = (
                    end_lines[d][e * 4:(e + 1) * 4, :]
                )
        else:
            for e in range(2):
                side_out[pl.ds(d * 4 * lay.side + lay.ends + 2 + e, 4, stride=lay.side), :] = (
                    jnp.zeros((4, LANES), F32)
                )
        for k in order:
            send(
                side_out.at[pl.ds((d * 4 + k) * lay.side, lay.side)], side_in.at[k, d],
                4 + d * 4 + k, d, k, target_of(d, k),
            )

    for f in range(fields):
        for corner in range(4):
            x = 0 if corner // 2 else edge - 1
            y = 0 if corner % 2 else edge - 1
            start = f * plane + x * edge + y
            corner_lines[7 - f, corner:corner + 1, :] = upd[start:start + 1, :]
    by_region = transposed_groups([corner_lines[f] for f in range(8)], edge)
    for k in range(4):
        region = corner_region[k]
        total = by_region[0]
        for g in range(1, 8):
            total = jnp.where(region == float(g), by_region[g], total)
        for corner in range(4):
            corner_out[corner, k] = total[corner:corner + 1, :]
    for corner in range(4):
        for k in order:
            send(
                corner_out.at[corner, k], corner_in.at[k, corner],
                20 + corner * 4 + k, 4 + corner, k, target_of(4 + corner, k),
            )

    for remote, local, itself in third:
        if local is None:
            remote.wait_recv()
        elif remote is None:
            local.wait()
        else:
            pl.when(itself)(local.wait)
            pl.when(jnp.logical_not(itself))(remote.wait_recv)

    for s in range(slots):
        delta = owner[0, s]
        k = delta + 2 - jnp.where(delta > 0, 1, 0)
        for d in range(4):
            window[s, d * lay.side:(d + 1) * lay.side, :] = side_in[k, d]
        window[s, lay.z:lay.z + z_size, :] = z_in[k]
        for corner in range(4):
            window[s, lay.corner + corner:lay.corner + corner + 1, :] = corner_in[k, corner]

    for copy in first + told + passed:
        copy.wait_send()
    for remote, local, itself in third:
        if local is None:
            remote.wait_send()
        elif remote is not None:
            pl.when(jnp.logical_not(itself))(remote.wait_send)


def ghost_kernel(
    slots, fields, edge, count, mask, window, updated_in, updated_out, ghost_out,
    ghost, pass_sem, out_sem,
):
    lay = Layout(fields, edge)
    live_count = count[0]
    outs = [pltpu.make_async_copy(updated_in, updated_out, pass_sem.at[0])]
    outs[0].start()

    def weights(width, target, along, within, normal):
        row = iota((LANES, width), 0)
        part = (row // edge) % 4
        signs = jnp.where(part == 1, along, jnp.where(part == 2, within, normal))
        value = jnp.where(part == 0, 1.0, jnp.where(signs == 1, 0.125, -0.125))
        return jnp.where(row % edge == target, value, 0.0).astype(BF16)

    lx = iota((LANES, 2 * LANES), 1)
    lz = iota((LANES, LANES), 1)
    quarter = 2 * edge
    tables = (
        weights(2 * LANES, (lx % quarter) // 2, (lx // quarter) % 2, lx % 2, lx // LANES),
        weights(LANES, (lz % quarter) // 2, lz // 64, lz % 2, (lz // quarter) % 2),
        weights(LANES, (lz % 64) // 4, lz // 64, (lz // 2) % 2, lz % 2),
    )
    lane = iota((SUB, LANES), 1)
    in_group = lane % edge
    last_lane, first_lane = lane >= LANES - edge, lane < edge
    low_half = lane < LANES // 2

    for s in range(slots):
        def rows(start):
            return window[s, start:start + SUB, :]

        def spread(start, shift, stride):
            row = jnp.broadcast_to(window[s, start:start + 1, :], (SUB, LANES))
            return pltpu.roll(row, shift % LANES, 1, stride=stride, stride_axis=0)

        for kind in range(3):
            parts = [[], [], [], []]
            for side in range(2):
                face = 2 * kind + side
                base = face * lay.side if kind < 2 else lay.z + side * 4 * fields
                centre = [rows(base + h * fields) for h in range(2)]
                far = [rows(base + (2 + h) * fields) for h in range(2)]
                own = [rows(lay.own + (2 * face + h) * fields) for h in range(2)]
                if kind == 0:
                    lines = [lay.corner + 2 * side, lay.corner + 2 * side + 1]
                elif kind == 1:
                    lines = [lay.corner + side, lay.corner + 2 + side]
                else:
                    lines = [d * lay.side + lay.ends + 2 + side for d in range(2)]
                below = spread(lines[0], edge, edge)
                above = spread(lines[1], 0, edge)
                up = [pltpu.roll(v, LANES - edge, 1) for v in centre]
                down = [pltpu.roll(v, edge, 1) for v in centre]
                along = [
                    jnp.where(last_lane, up[1], up[0]) - jnp.where(first_lane, below, down[0]),
                    jnp.where(last_lane, above, up[1]) - jnp.where(first_lane, down[0], down[1]),
                ]
                within = []
                for h in range(2):
                    if kind < 2:
                        before = spread(base + lay.ends + h, 1 - edge, 2)
                        after = spread(base + lay.ends + h, edge - 1, 2)
                    else:
                        low_row, high_row = 2 * lay.side + lay.ends + h, 3 * lay.side + lay.ends + h
                        before = spread(low_row, 0 if side else 1 - edge, 2)
                        after = spread(high_row, edge - 1 if side else 0, 2)
                    right = jnp.where(in_group == edge - 1, after, pltpu.roll(centre[h], LANES - 1, 1))
                    left = jnp.where(in_group == 0, before, pltpu.roll(centre[h], 1, 1))
                    within.append(right - left)
                normal = [(o - v) if side == 0 else (v - o) for o, v in zip(own, far)]
                for part, values in zip(parts, (centre, along, within, normal)):
                    part.extend(values)
            wide = [jnp.concatenate(part, axis=0) for part in parts]
            high = [v.astype(BF16).astype(F32) for v in wide]
            low = [v - u for v, u in zip(wide, high)]
            groups = transposed_groups(high + low, edge)
            spreads = jnp.dot(
                jnp.concatenate(groups, axis=0).astype(BF16), tables[kind], preferred_element_type=F32
            )
            for side in range(2):
                face = 2 * kind + side
                keep = jnp.where((s < live_count) & (mask[s, face] > 0), 1.0, 0.0).astype(F32)
                for h in range(2):
                    def cell(i):
                        start = (i * 4 + side * 2 + h) * SUB
                        return spreads[start:start + SUB, :]

                    if kind == 0:
                        for t in range(4):
                            for layer in range(2):
                                cols = slice(layer * LANES, (layer + 1) * LANES)
                                value = jnp.where(low_half, cell(2 * t)[:, cols], cell(2 * t + 1)[:, cols])
                                to = (layer * 8 + h * 4 + t) * LANES
                                ghost[s, :, face, to:to + LANES] = (value * keep)[:fields]
                    else:
                        for i in range(8):
                            to = (h * 8 + i) * LANES
                            ghost[s, :, face, to:to + LANES] = (cell(i) * keep)[:fields]
        outs.append(pltpu.make_async_copy(ghost.at[s], ghost_out.at[s], out_sem.at[s]))
        outs[-1].start()
    for copy in outs:
        copy.wait()


def body(n_box, n_lev, fine, coarse, owner_map, patch_count, face_mask):
    slots, fields, fine_edge, _ = fine.shape
    edge = fine_edge // 2
    block = fields * edge
    lay = Layout(fields, edge)
    vmem = pl.BlockSpec(memory_space=pltpu.VMEM)
    smem = pl.BlockSpec(memory_space=pltpu.SMEM)
    hbm = pl.BlockSpec(memory_space=pltpu.HBM)
    flat = jax.ShapeDtypeStruct((block * edge, LANES), F32)
    updated, window = pl.pallas_call(
        functools.partial(kernel, n_box, n_lev, slots, fields, edge),
        out_shape=(flat, jax.ShapeDtypeStruct((slots, lay.rows, LANES), F32)),
        in_specs=[smem, smem, hbm, hbm],
        out_specs=(vmem, vmem),
        scratch_shapes=[
            pltpu.VMEM((slots * fields * fine_edge, fine_edge * fine_edge), F32),
            pltpu.VMEM((block * edge, LANES), F32),
            pltpu.VMEM((slots * fields * fine_edge, LANES), F32),
            pltpu.VMEM((slots * fields * fine_edge, LANES), F32),
            pltpu.VMEM((2 * slots * block, LANES), F32),
            pltpu.VMEM((4 * slots * block, LANES), F32),
            pltpu.VMEM((4, block, 2 * LANES), F32),
            pltpu.VMEM((4, block, 2 * LANES), F32),
            pltpu.VMEM((4, 1, LANES), F32),
            pltpu.VMEM((4, 1, LANES), F32),
            pltpu.VMEM((8, 4, 1, LANES), F32),
            pltpu.VMEM((SUB * edge * edge, LANES), F32),
            pltpu.VMEM((SUB, SUB, LANES), F32),
            pltpu.VMEM((4, SUB, LANES), F32),
            pltpu.VMEM((16 * lay.side, LANES), F32),
            pltpu.VMEM((4, 4, lay.side, LANES), F32),
            pltpu.VMEM((4 * 8 * fields, LANES), F32),
            pltpu.VMEM((4, 8 * fields, LANES), F32),
            pltpu.VMEM((4, 4, 1, LANES), F32),
            pltpu.VMEM((4, 4, 1, LANES), F32),
            pltpu.VMEM((4, 2 * LANES, 2 * LANES), BF16),
            pltpu.SemaphoreType.DMA((2 * slots + 1,)),
            pltpu.SemaphoreType.DMA((8,)),
            pltpu.SemaphoreType.DMA((8,)),
            pltpu.SemaphoreType.DMA((12,)),
            pltpu.SemaphoreType.DMA((12,)),
            pltpu.SemaphoreType.DMA((36,)),
            pltpu.SemaphoreType.DMA((36,)),
        ],
        compiler_params=pltpu.CompilerParams(
            collective_id=0, has_side_effects=True, vmem_limit_bytes=55000000
        ),
    )(
        owner_map.T, patch_count,
        fine.reshape(slots * fields * fine_edge, fine_edge * fine_edge),
        coarse.reshape(block * edge, LANES),
    )
    ghost_shape = (slots, fields, 6, 2 * fine_edge * fine_edge)
    updated, ghost = pl.pallas_call(
        functools.partial(ghost_kernel, slots, fields, edge),
        out_shape=(flat, jax.ShapeDtypeStruct(ghost_shape, F32)),
        in_specs=[smem, smem, vmem, vmem],
        out_specs=(hbm, hbm),
        scratch_shapes=[
            pltpu.VMEM(ghost_shape, F32),
            pltpu.SemaphoreType.DMA((1,)),
            pltpu.SemaphoreType.DMA((slots,)),
        ],
        compiler_params=pltpu.CompilerParams(vmem_limit_bytes=16777216),
    )(patch_count, face_mask, window, updated)
    return updated.reshape(coarse.shape), ghost.transpose(0, 2, 1, 3)


def solution(mesh):
    return jax.shard_map(
        functools.partial(body, mesh.shape["box"], mesh.shape["lev"]),
        mesh=mesh,
        in_specs=(
            P(("box", "lev"), None, None, None),
            P(None, "box", "lev", None),
            P(("box", "lev"), None),
            P(("box", "lev")),
            P(("box", "lev"), None),
        ),
        out_specs=(P(None, "box", "lev", None), P(("box", "lev"), None, None, None)),
        check_vma=False,
    )
```

time: 29.6 us -> 29.2 us (0.986)
  Pallas kernels: 27.5 us -> 27.1 us
    pallas_call x1, Pallas kernels: 25 us -> 23.4 us  [body(): pl.pallas_call(functools.partial(kernel, n_box, n_lev, slots, fields, edg...]
    pallas_call x1, Pallas kernels: 2.42 us -> 3.67 us  [body(): pl.pallas_call(functools.partial(ghost_kernel, slots, fields, edge), out_...]
where the time goes in v2:
time: 29.2 us; the launch traced here: 29.1 us
  Pallas kernels  27.1 us (93%)
  between operations  1.32 us (5%)
  local copies, waits for them, and re-layouts  0.68 us (2%)
    pallas_call x1, Pallas kernels, body(): pl.pallas_call(functools.partial(kernel, n_box, n_lev, slots, fields, edg...  23.4 us
    pallas_call x1, Pallas kernels, body(): pl.pallas_call(functools.partial(ghost_kernel, slots, fields, edge), out_...  3.67 us
    unnamed x4, local copies, waits for them, and re-layouts  0.68 us

profile of v2, /device:TPU:0, one launch (start us, length us, event | category | flops | bytes accessed | tf_op | source)
XLA Modules:
  0.0 29.1 jit_solution(8811100667421955301)
XLA Ops:
  0.6 0.0 copy-start
  1.3 0.0 copy-start.1
  1.3 0.7 %copy-done.1 = s32[3,2]{0,1:T(2,128)S(1)} copy-done((s32[3,2]{0,1:T(2,128)S(1)}, s32[3,2]{0,1:T(2,128)}, u32[]{:S(2)}) %copy-start.1) | copy-done | bytes 48
  2.0 23.4 %shard_map.68 = (f32[1280,128]{1,0:T(8,128)S(1)}, f32[3,216,128]{2,1,0:T(8,128)S(1)}) custom-call(s32[2,3]{1,0:T(2,128)S(1)} %bitcast.5, s32[1]{0:T(128)S(6)} %copy.7.count, f32[480,1024]{1,0:T(8,128)} %bitcast.6, f32[1280,128]{1,0:T(8,128)} %bitcast.7), custom_call_target="tpu_custom_call" | custom-call | tf_op jit(solution)/shard_map/pallas_call | solution.py:568
  25.4 0.0 copy-done
  25.4 3.7 %shard_map.69 = (f32[1280,128]{1,0:T(8,128)}, f32[3,5,6,2048]{3,2,1,0:T(8,128)}) custom-call(s32[1]{0:T(128)S(6)} %copy.7.count, s32[3,6]{1,0:T(4,128)S(1)} %copy-done, f32[3,216,128]{2,1,0:T(8,128)S(1)} %get-tuple-element.6.window, f32[1280,128]{1,0:T(8,128)S(1)} %get-tuple-element.7.updated_in), custom_call_target="tpu_custom_call" | custom-call | tf_op jit(solution)/shard_map/pallas_call | solution.py:612
Async XLA Ops:
  0.6 24.8 %copy-start = (s32[3,6]{1,0:T(4,128)S(1)}, s32[3,6]{1,0:T(4,128)}, u32[]{:S(2)}) copy-start(s32[3,6]{1,0:T(4,128)} %mask.1) | copy-start | bytes 220
  1.3 0.7 %copy-start.1 = (s32[3,2]{0,1:T(2,128)S(1)}, s32[3,2]{0,1:T(2,128)}, u32[]{:S(2)}) copy-start(s32[3,2]{0,1:T(2,128)} %param.7) | copy-start | bytes 76

commit v3 on v2

--- a/solution.py
+++ b/solution.py
@@ -13,6 +13,8 @@
 F32 = jnp.float32
 BF16 = jnp.bfloat16
 MESH_ID = pl.DeviceIdType.MESH
+VMEM_FIRST = 56000000
+VMEM_SECOND = 56000000
 
 
 def iota(shape, dim):
@@ -53,18 +55,17 @@
     def __init__(self, fields, edge):
         self.ends = 4 * fields
         self.side = 4 * fields + 4
+        self.z_size = 8 * fields
         self.z = 4 * self.side
-        self.corner = self.z + 8 * fields
-        self.own = self.corner + 8
-        self.rows = self.own + 12 * fields + 8
+        self.corner = self.z + self.z_size
+        self.own = self.corner + 4
+        self.keep = self.own + 12 * fields
+        self.rows = self.keep + 6
         self.rows = self.rows + (-self.rows) % SUB
+        self.field = edge * edge + SUB
 
 
 DIRECTIONS = ((-1, 0), (1, 0), (0, -1), (0, 1), (-1, -1), (-1, 1), (1, -1), (1, 1))
-
-
-def opposite(d):
-    return d ^ 1 if d < 4 else 11 - d
 
 
 def relations(n_box, n_lev):
@@ -88,16 +89,16 @@
                 add(target)
                 same.setdefault((d, k), set()).add(target == me)
     offsets.discard((0, 0))
-    return sorted(offsets), same
+    reach = max(min(db, n_box - db) for db, _ in offsets)
+    return sorted(offsets), reach, same
 
 
 def kernel(
     n_box, n_lev, slots, fields, edge,
-    owner, count, fine_far, coarse_far, updated, window,
-    fine, coarse, half_a, half_b, avg, own_got, send1, recv1, region_out, region_in, near_in,
-    upd, corner_lines, corner_region, side_out, side_in, z_out, z_in, corner_out, corner_in,
-    place_table,
-    load, s1, r1, sh, rh, s3, r3,
+    owner_far, count_far, mask_far, fine_far, coarse_far, updated, window,
+    owner_of, count, mask, fine, coarse, avg, own_got, send1, recv1, region_out, near_in,
+    upd, corner_lines, corner_region, side_out, side_in, z_out, z_in, corner_out, corner_in, place_table,
+    small, load, put, s1, r1, sh, rh, s3, r3, mixed,
 ):
     fine_edge = 2 * edge
     block = fields * edge
@@ -106,18 +107,30 @@
     frows = fields * fine_edge
     cut = (fields + 1) // 2
     chunks = ((0, cut), (cut, fields))
+    small_loads = [
+        pltpu.make_async_copy(src, dst, small.at[i])
+        for i, (src, dst) in enumerate(((owner_far, owner_of), (count_far, count), (mask_far, mask)))
+    ]
+    for copy in small_loads:
+        copy.start()
+    all_rows = slots * frows
     loads = {}
     for part, (f0, f1) in enumerate(chunks):
         for s in range(slots):
-            rows = pl.ds(s * frows + f0 * fine_edge, (f1 - f0) * fine_edge)
-            loads[part, s] = pltpu.make_async_copy(
-                fine_far.at[rows], fine.at[rows], load.at[part * slots + s]
-            )
-            loads[part, s].start()
-    coarse_load = pltpu.make_async_copy(coarse_far, coarse, load.at[2 * slots])
+            start, size = s * frows + f0 * fine_edge, (f1 - f0) * fine_edge
+            for t in range(8):
+                copy = pltpu.make_async_copy(
+                    fine_far.at[pl.ds(start, size), pl.ds(t * LANES, LANES)],
+                    fine.at[pl.ds(t * all_rows + start, size)],
+                    load.at[part],
+                )
+                copy.start()
+        rows = fine.at[pl.ds(0, 8 * slots * (f1 - f0) * fine_edge)]
+        loads[part] = pltpu.make_async_copy(rows, rows, load.at[part])
+    coarse_load = pltpu.make_async_copy(coarse_far, coarse, small.at[3])
     coarse_load.start()
     n_dev = n_box * n_lev
-    offsets, same = relations(n_box, n_lev)
+    offsets, reach, same = relations(n_box, n_lev)
     box = lax.axis_index("box")
     lev = lax.axis_index("lev")
     me = box * n_lev + lev
@@ -131,45 +144,65 @@
     def beside(dx, dy):
         return (lax.rem(box + (dx + n_box), n_box), lax.rem(lev + (dy + n_lev), n_lev))
 
-    around = [beside(dx, dy) for dx, dy in DIRECTIONS]
     barrier = pltpu.get_barrier_semaphore()
     for db, dl in offsets:
         pl.semaphore_signal(barrier, inc=1, device_id=beside(db, dl), device_id_type=MESH_ID)
 
+    q = iota((fine_edge * fine_edge, plane), 0)
+    c = iota((fine_edge * fine_edge, plane), 1)
+    goal = (q // (2 * fine_edge)) * edge + (q % fine_edge) // 2
+    table = jnp.where(goal == c, 0.125, 0.0).astype(BF16)
+    order = (1, 2, 0, 3)
+    back = [shifted(-delta) for delta in DELTAS]
+
+    def target_of(d, k):
+        dx, dy = DIRECTIONS[d]
+        other = beside(-dx, -dy)
+        return at(lax.rem(other[0] * n_lev + other[1] + (n_dev - DELTAS[k]), n_dev))
+
+    targets = [[target_of(d, k) for k in range(4)] for d in range(8)]
+
+    def place_of(device):
+        db = lax.rem(device[0] - box + (n_box + reach), n_box)
+        return db * n_lev + lax.rem(device[1] - lev + n_lev, n_lev)
+
+    for copy in small_loads:
+        copy.wait()
     live_count = count[0]
+    owner = [owner_of[0, s] for s in range(slots)]
+    region_of = [owner_of[1, s] for s in range(slots)]
     chosen = [
-        [(s < live_count) & (owner[0, s] == delta) for delta in DELTAS] for s in range(slots)
+        [(s < live_count) & (owner[s] == delta) for delta in DELTAS] for s in range(slots)
     ]
     weight = [[jnp.where(c, 1.0, 0.0).astype(F32) for c in row] for row in chosen]
     for k in range(4):
         region = jnp.int32(-1)
         for s in range(slots):
-            region = jnp.where(chosen[s][k], owner[1, s], region)
+            region = jnp.where(chosen[s][k], region_of[s], region)
         region_out[k] = jnp.full((1, LANES), 1.0, F32) * region.astype(F32)
 
-    q = iota((fine_edge * fine_edge, plane), 0)
-    c = iota((fine_edge * fine_edge, plane), 1)
-    goal = (q // (2 * fine_edge)) * edge + (q % fine_edge) // 2
-    table = jnp.where(goal == c, 0.125, 0.0).astype(BF16)
-    first, told = [], []
-    order = (1, 2, 0, 3)
+    near_in[reach * n_lev] = region_out[...]
+    first = {}
     for part, (f0, f1) in enumerate(chunks):
         size = (f1 - f0) * edge
-        for s in range(slots):
-            loads[part, s].wait()
-            rows = slice(s * frows + f0 * fine_edge, s * frows + f1 * fine_edge)
-            high, low = split(fine[rows, :])
-            got = jnp.dot(high, table, preferred_element_type=F32) + jnp.dot(
-                low, table, preferred_element_type=F32
-            )
-            half_a[rows, :] = got[:, :LANES]
-            half_b[rows, :] = got[:, LANES:]
+        loads[part].wait()
+        columns = []
+        for t in range(8):
+            pieces = []
+            for s in range(slots):
+                start = t * all_rows + s * frows + f0 * fine_edge
+                pieces.append(
+                    fine[pl.ds(start, size, stride=2), :] + fine[pl.ds(start + 1, size, stride=2), :]
+                )
+            columns.append(jnp.concatenate(pieces, axis=0))
+        high, low = split(jnp.concatenate(columns, axis=1))
+        got = jnp.dot(jnp.concatenate([high, low], axis=0), table, preferred_element_type=F32)
+        got = got[:slots * size] + got[slots * size:]
         to = f0 * edge
-        for h, half in enumerate((half_a, half_b)):
+        for h in range(2):
             averaged = []
             for s in range(slots):
-                start = s * frows + f0 * fine_edge
-                mean = half[pl.ds(start, size, stride=2), :] + half[pl.ds(start + 1, size, stride=2), :]
+                mean = got[s * size:(s + 1) * size, h * LANES:(h + 1) * LANES]
                 start = (h * slots + s) * block + to
                 avg[start:start + size, :] = mean
                 averaged.append(mean)
@@ -180,34 +213,23 @@
                 send1[k, to:to + size, h * LANES:(h + 1) * LANES] = total
         if part == 0:
             pl.semaphore_wait(barrier, len(offsets))
-            for k in order:
+            for db, dl in offsets:
+                slot = ((reach - db) % n_box) * n_lev + (-dl) % n_lev
                 copy = pltpu.make_async_remote_copy(
-                    src_ref=region_out.at[k], dst_ref=region_in.at[k],
-                    send_sem=sh.at[k], recv_sem=rh.at[k],
-                    device_id=shifted(DELTAS[k]), device_id_type=MESH_ID,
+                    src_ref=region_out, dst_ref=near_in.at[slot],
+                    send_sem=sh.at[0], recv_sem=rh.at[0],
+                    device_id=beside(db, dl), device_id_type=MESH_ID,
                 )
                 copy.start()
-                told.append(copy)
         for k in order:
             copy = pltpu.make_async_remote_copy(
                 src_ref=send1.at[k, pl.ds(to, size)], dst_ref=recv1.at[k, pl.ds(to, size)],
-                send_sem=s1.at[part * 4 + k], recv_sem=r1.at[part * 4 + k],
+                send_sem=s1.at[0], recv_sem=r1.at[part],
                 device_id=shifted(DELTAS[k]), device_id_type=MESH_ID,
             )
             copy.start()
-            first.append(copy)
-
-    for copy in told:
-        copy.wait_recv()
-    passed = []
-    for d in range(8):
-        copy = pltpu.make_async_remote_copy(
-            src_ref=region_in, dst_ref=near_in.at[opposite(d)],
-            send_sem=sh.at[4 + d], recv_sem=rh.at[4 + opposite(d)],
-            device_id=around[d], device_id_type=MESH_ID,
-        )
-        copy.start()
-        passed.append(copy)
+        rows = recv1.at[:, pl.ds(to, size)]
+        first[part] = pltpu.make_async_copy(rows, rows, r1.at[part])
 
     for pair in range(4):
         row = iota((LANES, 2 * LANES), 0)
@@ -248,13 +270,17 @@
                 to = lay.own + (2 * (2 + kind) + h) * fields
                 window[s, to:to + fields, :] = total
 
+        for face in range(6):
+            keep = jnp.where((s < live_count) & (mask[s, face] > 0), 1.0, 0.0).astype(F32)
+            window[s, lay.keep + face:lay.keep + face + 1, :] = jnp.full((1, LANES), 1.0, F32) * keep
     corner_lines[...] = jnp.zeros_like(corner_lines)
     coarse_load.wait()
-    for copy in passed:
-        copy.wait_recv()
+    told = near_in.at[pl.ds(0, len(offsets))]
+    pltpu.make_async_copy(told, told, rh.at[0]).wait()
 
     lane = iota((1, LANES), 1).astype(F32)
-    here_rows = [region_in[k] for k in range(4)]
+    here_rows = [near_in[place_of(back[k]), k] for k in range(4)]
+    near = [[near_in[place_of(targets[d][k]), k] for k in range(4)] for d in range(8)]
 
     def pick(region, place):
         t = lane - edge * region - place
@@ -265,15 +291,15 @@
         for k in range(4):
             for place in (-1 - depth, edge + depth):
                 z_rows.append(pick(here_rows[k], place))
-    for d in (1, 0):
+    for d in range(2):
         for place in (-1, edge):
             for k in range(4):
-                z_rows.append(pick(near_in[d, k], place))
+                z_rows.append(pick(near[d][k], place))
     z_table = jnp.concatenate(z_rows, axis=0).astype(BF16)
     z_table = jnp.concatenate([z_table, z_table], axis=1)
     for corner in range(4):
         for k in range(4):
-            corner_region[k, corner:corner + 1, :] = near_in[opposite(4 + corner), k]
+            corner_region[k, corner:corner + 1, :] = near[4 + corner][k]
 
     group = (iota((1, LANES), 1) // edge).astype(F32)
     here = [group == region for region in here_rows]
@@ -281,8 +307,7 @@
     end_lines = [jnp.zeros((SUB, LANES), F32) for _ in range(2)]
     for part, (f0, f1) in enumerate(chunks):
         size = (f1 - f0) * edge
-        for k in range(4):
-            first[part * 4 + k].wait_recv()
+        first[part].wait()
         to = f0 * edge
         for h in range(2):
             stacked = split_lanes(jnp.concatenate(
@@ -292,16 +317,23 @@
                 spread = jnp.dot(stacked, place_table[pair], preferred_element_type=F32)
                 for odd in range(2):
                     y = h * SUB + 2 * pair + odd
-                    rows = pl.ds(f0 * plane + y, size, stride=edge)
-                    merged = coarse[rows, :]
-                    for k in range(4):
-                        merged = jnp.where(
-                            here[k], spread[k * size:(k + 1) * size, odd * LANES:(odd + 1) * LANES], merged
-                        )
-                    upd[rows, :] = merged
-                    updated[rows, :] = merged
+                    for f in range(f0, f1):
+                        merged = coarse[pl.ds(f * plane + y, edge, stride=edge), :]
+                        for k in range(4):
+                            start = k * size + (f - f0) * edge
+                            merged = jnp.where(
+                                here[k],
+                                spread[start:start + edge, odd * LANES:(odd + 1) * LANES],
+                                merged,
+                            )
+                        upd[pl.ds(f * lay.field + y, edge, stride=edge), :] = merged
         for f in range(f0, f1):
-            got = times_transposed(z_table, split_lanes(upd[f * plane:(f + 1) * plane, :]))
+            pltpu.make_async_copy(
+                upd.at[pl.ds(f * lay.field, plane)], updated.at[pl.ds(f * plane, plane)], put.at[0]
+            ).start()
+        for f in range(f0, f1):
+            start = f * lay.field
+            got = times_transposed(z_table, split_lanes(upd[start:start + plane, :]))
             for depth in range(2):
                 for h in range(2):
                     z_out[pl.ds((2 * depth + h) * fields + f, 8, stride=4 * fields), :] = got[
@@ -314,38 +346,33 @@
             end_lines[0] = jnp.where(group8 == 7 - f, high_end, end_lines[0])
             end_lines[1] = jnp.where(group8 == 7 - f, low_end, end_lines[1])
 
-    third = []
-
-    def send(src, dst, slot, d, k, target):
+    clear, unclear = [0, 0, 0], []
+
+    def send(src, dst, sem, d, k, target):
         kinds = {False} if d is None else same[d, k]
-        remote = local = itself = None
+        remote = local = None
         if False in kinds:
             remote = pltpu.make_async_remote_copy(
-                src_ref=src, dst_ref=dst, send_sem=s3.at[slot], recv_sem=r3.at[slot],
-                device_id=target, device_id_type=MESH_ID,
+                src_ref=src, dst_ref=dst, recv_sem=r3.at[sem], device_id=target, device_id_type=MESH_ID,
+                send_sem=s3.at[sem] if len(kinds) == 1 else mixed.at[len(unclear)],
             )
         if True in kinds:
-            local = pltpu.make_async_copy(src, dst, r3.at[slot])
+            local = pltpu.make_async_copy(src, dst, r3.at[sem])
         if local is None:
             remote.start()
+            clear[sem] += 1
         elif remote is None:
             local.start()
         else:
             itself = (target[0] == box) & (target[1] == lev)
             pl.when(itself)(local.start)
             pl.when(jnp.logical_not(itself))(remote.start)
-        third.append((remote, local, itself))
-
-    def target_of(d, k):
-        other = around[opposite(d)]
-        linear = other[0] * n_lev + other[1]
-        return at(lax.rem(linear + (n_dev - DELTAS[k]), n_dev))
-
-    z_size = 8 * fields
+            unclear.append((remote, itself))
+
     for k in order:
-        send(z_out.at[pl.ds(k * z_size, z_size)], z_in.at[k], k, None, k, shifted(-DELTAS[k]))
-
-    field_step = plane
+        send(z_out.at[pl.ds(k * lay.z_size, lay.z_size)], z_in.at[k], 0, None, k, back[k])
+
+    field_step = lay.field
     sublane = iota((SUB, LANES), 0)
     in_group = iota((SUB, LANES), 1) % edge
     for d in (0, 1, 2, 3):
@@ -365,7 +392,7 @@
             after = by_region[(g + 1) % 8][:2 * SUB]
             ends.append(jnp.where(iota((2 * SUB, LANES), 1) % edge == 0, after, before))
         for k in range(4):
-            region = near_in[opposite(d), k]
+            region = near[d][k]
             total = by_region[0]
             end = ends[0]
             for g in range(1, 8):
@@ -380,9 +407,10 @@
             for h in range(2):
                 used = (sublane < fields) & ((in_group == 0) | (in_group == edge - 1))
                 one = jnp.where(used, end[h * SUB:(h + 1) * SUB, :], 0.0)
-                for bit in (1, 2, 4):
-                    moved = pltpu.roll(one, LANES - 2 * bit, 1)
-                    one = jnp.where((sublane // bit) % 2 == 1, moved, one)
+                moved = one
+                for f in range(1, fields):
+                    moved = jnp.where(sublane == f, pltpu.roll(one, LANES - 2 * f, 1), moved)
+                one = moved
                 side_out[base + lay.ends + h:base + lay.ends + h + 1, :] = jnp.sum(
                     one, axis=0, keepdims=True
                 )
@@ -396,17 +424,12 @@
                 side_out[pl.ds(d * 4 * lay.side + lay.ends + 2 + e, 4, stride=lay.side), :] = (
                     jnp.zeros((4, LANES), F32)
                 )
-        for k in order:
-            send(
-                side_out.at[pl.ds((d * 4 + k) * lay.side, lay.side)], side_in.at[k, d],
-                4 + d * 4 + k, d, k, target_of(d, k),
-            )
 
     for f in range(fields):
         for corner in range(4):
             x = 0 if corner // 2 else edge - 1
             y = 0 if corner % 2 else edge - 1
-            start = f * plane + x * edge + y
+            start = f * lay.field + x * edge + y
             corner_lines[7 - f, corner:corner + 1, :] = upd[start:start + 1, :]
     by_region = transposed_groups([corner_lines[f] for f in range(8)], edge)
     for k in range(4):
@@ -415,49 +438,49 @@
         for g in range(1, 8):
             total = jnp.where(region == float(g), by_region[g], total)
         for corner in range(4):
-            corner_out[corner, k] = total[corner:corner + 1, :]
+            corner_out[corner * 4 + k] = total[corner:corner + 1, :]
+    for d in (0, 1, 2, 3):
+        for k in order:
+            send(
+                side_out.at[pl.ds((d * 4 + k) * lay.side, lay.side)], side_in.at[k, d],
+                1, d, k, targets[d][k],
+            )
     for corner in range(4):
         for k in order:
             send(
-                corner_out.at[corner, k], corner_in.at[k, corner],
-                20 + corner * 4 + k, 4 + corner, k, target_of(4 + corner, k),
+                corner_out.at[corner * 4 + k], corner_in.at[k * 4 + corner],
+                2, 4 + corner, k, targets[4 + corner][k],
             )
 
-    for remote, local, itself in third:
-        if local is None:
-            remote.wait_recv()
-        elif remote is None:
-            local.wait()
-        else:
-            pl.when(itself)(local.wait)
-            pl.when(jnp.logical_not(itself))(remote.wait_recv)
-
+    for sem, ref in enumerate((z_in, side_in, corner_in)):
+        pltpu.make_async_copy(ref, ref, r3.at[sem]).wait()
     for s in range(slots):
-        delta = owner[0, s]
-        k = delta + 2 - jnp.where(delta > 0, 1, 0)
+        k = owner[s] + 2 - jnp.where(owner[s] > 0, 1, 0)
         for d in range(4):
             window[s, d * lay.side:(d + 1) * lay.side, :] = side_in[k, d]
-        window[s, lay.z:lay.z + z_size, :] = z_in[k]
+        window[s, lay.z:lay.z + lay.z_size, :] = z_in[k]
         for corner in range(4):
-            window[s, lay.corner + corner:lay.corner + corner + 1, :] = corner_in[k, corner]
-
-    for copy in first + told + passed:
-        copy.wait_send()
-    for remote, local, itself in third:
-        if local is None:
-            remote.wait_send()
-        elif remote is not None:
-            pl.when(jnp.logical_not(itself))(remote.wait_send)
+            window[s, lay.corner + corner:lay.corner + corner + 1, :] = corner_in[k * 4 + corner]
+
+    pltpu.make_async_copy(updated, updated, put.at[0]).wait()
+    pltpu.make_async_copy(send1, send1, s1.at[0]).wait()
+    told = near_in.at[pl.ds(0, len(offsets))]
+    pltpu.make_async_copy(told, told, sh.at[0]).wait()
+    for sem, (ref, size) in enumerate(((z_out, lay.z_size), (side_out, lay.side), (corner_out, 1))):
+        if clear[sem]:
+            rows = ref.at[pl.ds(0, clear[sem] * size)]
+            pltpu.make_async_copy(rows, rows, s3.at[sem]).wait()
+    for remote, itself in unclear:
+        pl.when(jnp.logical_not(itself))(remote.wait_send)
 
 
 def ghost_kernel(
-    slots, fields, edge, count, mask, window, updated_in, updated_out, ghost_out,
-    ghost, pass_sem, out_sem,
+    slots, fields, edge, updated_in, window, updated_out, ghost_out, passing, ghost, lhs, pass_sem, out_sem
 ):
     lay = Layout(fields, edge)
-    live_count = count[0]
-    outs = [pltpu.make_async_copy(updated_in, updated_out, pass_sem.at[0])]
-    outs[0].start()
+    into = pltpu.make_async_copy(updated_in, passing, pass_sem.at[0])
+    out = pltpu.make_async_copy(passing, updated_out, pass_sem.at[1])
+    into.start()
 
     def weights(width, target, along, within, normal):
         row = iota((LANES, width), 0)
@@ -480,11 +503,11 @@
     low_half = lane < LANES // 2
 
     for s in range(slots):
-        def rows(start):
-            return window[s, start:start + SUB, :]
+        def rows(start, size=SUB):
+            return window[s, start:start + size, :]
 
         def spread(start, shift, stride):
-            row = jnp.broadcast_to(window[s, start:start + 1, :], (SUB, LANES))
+            row = jnp.broadcast_to(rows(start, 1), (SUB, LANES))
             return pltpu.roll(row, shift % LANES, 1, stride=stride, stride_axis=0)
 
         for kind in range(3):
@@ -492,8 +515,8 @@
             for side in range(2):
                 face = 2 * kind + side
                 base = face * lay.side if kind < 2 else lay.z + side * 4 * fields
-                centre = [rows(base + h * fields) for h in range(2)]
-                far = [rows(base + (2 + h) * fields) for h in range(2)]
+                layers = [rows(base + h * fields) for h in range(4)]
+                centre, far = layers[:2], layers[2:]
                 own = [rows(lay.own + (2 * face + h) * fields) for h in range(2)]
                 if kind == 0:
                     lines = [lay.corner + 2 * side, lay.corner + 2 * side + 1]
@@ -528,12 +551,16 @@
             high = [v.astype(BF16).astype(F32) for v in wide]
             low = [v - u for v, u in zip(wide, high)]
             groups = transposed_groups(high + low, edge)
-            spreads = jnp.dot(
-                jnp.concatenate(groups, axis=0).astype(BF16), tables[kind], preferred_element_type=F32
-            )
+            lhs[s * 3 + kind] = jnp.concatenate(groups, axis=0).astype(BF16)
+
+    into.wait()
+    out.start()
+    for s in range(slots):
+        for kind in range(3):
+            spreads = jnp.dot(lhs[s * 3 + kind], tables[kind], preferred_element_type=F32)
             for side in range(2):
                 face = 2 * kind + side
-                keep = jnp.where((s < live_count) & (mask[s, face] > 0), 1.0, 0.0).astype(F32)
+                keep = window[s, lay.keep + face:lay.keep + face + 1, :]
                 for h in range(2):
                     def cell(i):
                         start = (i * 4 + side * 2 + h) * SUB
@@ -550,10 +577,9 @@
                         for i in range(8):
                             to = (h * 8 + i) * LANES
                             ghost[s, :, face, to:to + LANES] = (cell(i) * keep)[:fields]
-        outs.append(pltpu.make_async_copy(ghost.at[s], ghost_out.at[s], out_sem.at[s]))
-        outs[-1].start()
-    for copy in outs:
-        copy.wait()
+        pltpu.make_async_copy(ghost.at[s], ghost_out.at[s], out_sem.at[0]).start()
+    out.wait()
+    pltpu.make_async_copy(ghost, ghost_out, out_sem.at[0]).wait()
 
 
 def body(n_box, n_lev, fine, coarse, owner_map, patch_count, face_mask):
@@ -561,50 +587,58 @@
     edge = fine_edge // 2
     block = fields * edge
     lay = Layout(fields, edge)
+    offsets, reach, same = relations(n_box, n_lev)
+    far = pl.BlockSpec(memory_space=pl.ANY)
     vmem = pl.BlockSpec(memory_space=pltpu.VMEM)
-    smem = pl.BlockSpec(memory_space=pltpu.SMEM)
-    hbm = pl.BlockSpec(memory_space=pltpu.HBM)
     flat = jax.ShapeDtypeStruct((block * edge, LANES), F32)
+    places = (2 * reach + 1) * n_lev
+    owner_rows = owner_map.T
     updated, window = pl.pallas_call(
         functools.partial(kernel, n_box, n_lev, slots, fields, edge),
-        out_shape=(flat, jax.ShapeDtypeStruct((slots, lay.rows, LANES), F32)),
-        in_specs=[smem, smem, hbm, hbm],
-        out_specs=(vmem, vmem),
+        out_shape=(
+            flat,
+            jax.ShapeDtypeStruct((slots, lay.rows, LANES), F32),
+        ),
+        in_specs=[far] * 5,
+        out_specs=(far, vmem),
         scratch_shapes=[
-            pltpu.VMEM((slots * fields * fine_edge, fine_edge * fine_edge), F32),
+            pltpu.SMEM(owner_rows.shape, jnp.int32),
+            pltpu.SMEM(patch_count.shape, jnp.int32),
+            pltpu.SMEM(face_mask.shape, jnp.int32),
+            pltpu.VMEM((8 * slots * fields * fine_edge, LANES), F32),
             pltpu.VMEM((block * edge, LANES), F32),
-            pltpu.VMEM((slots * fields * fine_edge, LANES), F32),
-            pltpu.VMEM((slots * fields * fine_edge, LANES), F32),
             pltpu.VMEM((2 * slots * block, LANES), F32),
             pltpu.VMEM((4 * slots * block, LANES), F32),
             pltpu.VMEM((4, block, 2 * LANES), F32),
             pltpu.VMEM((4, block, 2 * LANES), F32),
             pltpu.VMEM((4, 1, LANES), F32),
-            pltpu.VMEM((4, 1, LANES), F32),
-            pltpu.VMEM((8, 4, 1, LANES), F32),
-            pltpu.VMEM((SUB * edge * edge, LANES), F32),
+            pltpu.VMEM((places, 4, 1, LANES), F32),
+            pltpu.VMEM((SUB * lay.field, LANES), F32),
             pltpu.VMEM((SUB, SUB, LANES), F32),
             pltpu.VMEM((4, SUB, LANES), F32),
             pltpu.VMEM((16 * lay.side, LANES), F32),
             pltpu.VMEM((4, 4, lay.side, LANES), F32),
-            pltpu.VMEM((4 * 8 * fields, LANES), F32),
-            pltpu.VMEM((4, 8 * fields, LANES), F32),
-            pltpu.VMEM((4, 4, 1, LANES), F32),
-            pltpu.VMEM((4, 4, 1, LANES), F32),
+            pltpu.VMEM((4 * lay.z_size, LANES), F32),
+            pltpu.VMEM((4, lay.z_size, LANES), F32),
+            pltpu.VMEM((16, 1, LANES), F32),
+            pltpu.VMEM((16, 1, LANES), F32),
             pltpu.VMEM((4, 2 * LANES, 2 * LANES), BF16),
-            pltpu.SemaphoreType.DMA((2 * slots + 1,)),
-            pltpu.SemaphoreType.DMA((8,)),
-            pltpu.SemaphoreType.DMA((8,)),
-            pltpu.SemaphoreType.DMA((12,)),
-            pltpu.SemaphoreType.DMA((12,)),
-            pltpu.SemaphoreType.DMA((36,)),
-            pltpu.SemaphoreType.DMA((36,)),
+            pltpu.SemaphoreType.DMA((4,)),
+            pltpu.SemaphoreType.DMA((2,)),
+            pltpu.SemaphoreType.DMA((1,)),
+            pltpu.SemaphoreType.DMA((1,)),
+            pltpu.SemaphoreType.DMA((2,)),
+            pltpu.SemaphoreType.DMA((1,)),
+            pltpu.SemaphoreType.DMA((1,)),
+            pltpu.SemaphoreType.DMA((3,)),
+            pltpu.SemaphoreType.DMA((3,)),
+            pltpu.SemaphoreType.DMA((max(1, sum(len(v) > 1 for v in same.values())),)),
         ],
         compiler_params=pltpu.CompilerParams(
-            collective_id=0, has_side_effects=True, vmem_limit_bytes=55000000
+            collective_id=0, has_side_effects=True, vmem_limit_bytes=VMEM_FIRST
         ),
     )(
-        owner_map.T, patch_count,
+        owner_rows, patch_count, face_mask,
         fine.reshape(slots * fields * fine_edge, fine_edge * fine_edge),
         coarse.reshape(block * edge, LANES),
     )
@@ -612,15 +646,17 @@
     updated, ghost = pl.pallas_call(
         functools.partial(ghost_kernel, slots, fields, edge),
         out_shape=(flat, jax.ShapeDtypeStruct(ghost_shape, F32)),
-        in_specs=[smem, smem, vmem, vmem],
-        out_specs=(hbm, hbm),
+        in_specs=[far, vmem],
+        out_specs=(far, far),
         scratch_shapes=[
+            pltpu.VMEM((block * edge, LANES), F32),
             pltpu.VMEM(ghost_shape, F32),
+            pltpu.VMEM((3 * slots, 2 * LANES, LANES), BF16),
+            pltpu.SemaphoreType.DMA((2,)),
             pltpu.SemaphoreType.DMA((1,)),
-            pltpu.SemaphoreType.DMA((slots,)),
         ],
-        compiler_params=pltpu.CompilerParams(vmem_limit_bytes=16777216),
-    )(patch_count, face_mask, window, updated)
+        compiler_params=pltpu.CompilerParams(vmem_limit_bytes=VMEM_SECOND),
+    )(updated, window)
     return updated.reshape(coarse.shape), ghost.transpose(0, 2, 1, 3)
 
 

time: 29.2 us -> 26.5 us (0.908)
  Pallas kernels: 27.1 us -> 23.6 us
  local copies, waits for them, and re-layouts: 0.68 us -> 1.35 us
    pallas_call x1, Pallas kernels: 23.4 us -> 19 us  [body(): pl.pallas_call(functools.partial(kernel, n_box, n_lev, slots, fields, edg...]
    pallas_call x1, Pallas kernels: 3.67 us -> 4.61 us  [body(): pl.pallas_call(functools.partial(ghost_kernel, slots, fields, edge), out_...]
    unnamed x4, local copies, waits for them, and re-layouts: 0.68 us -> 1.35 us
where the time goes in v3:
time: 26.5 us; the launch traced here: 26.2 us
  Pallas kernels  23.6 us (89%)
  local copies, waits for them, and re-layouts  1.35 us (5%)
  between operations  1.29 us (5%)
    pallas_call x1, Pallas kernels, body(): pl.pallas_call(functools.partial(kernel, n_box, n_lev, slots, fields, edg...  19 us
    pallas_call x1, Pallas kernels, body(): pl.pallas_call(functools.partial(ghost_kernel, slots, fields, edge), out_...  4.61 us
    unnamed x4, local copies, waits for them, and re-layouts  1.35 us

profile of v3, /device:TPU:0, one launch (start us, length us, event | category | flops | bytes accessed | tf_op | source)
XLA Modules:
  0.0 26.2 jit_solution(4481140114959874059)
XLA Ops:
  1.3 0.0 copy-start
  1.3 0.7 %copy-done = s32[3,6]{1,0:T(4,128)S(1)} copy-done((s32[3,6]{1,0:T(4,128)S(1)}, s32[3,6]{1,0:T(4,128)}, u32[]{:S(2)}) %copy-start) | copy-done | bytes 96
  2.0 0.0 copy-start.1
  2.0 0.7 %copy-done.1 = s32[3,2]{0,1:T(2,128)S(1)} copy-done((s32[3,2]{0,1:T(2,128)S(1)}, s32[3,2]{0,1:T(2,128)}, u32[]{:S(2)}) %copy-start.1) | copy-done | bytes 48
  2.6 19.0 %shard_map.68 = (f32[1280,128]{1,0:T(8,128)}, f32[3,208,128]{2,1,0:T(8,128)S(1)}) custom-call(s32[2,3]{1,0:T(2,128)S(1)} %bitcast.5, s32[1]{0:T(128)S(6)} %copy.7.count_far, s32[3,6]{1,0:T(4,128)S(1)} %copy-done, f32[480,1024]{1,0:T(8,128)} %bitcast.6, f32[1280,128]{1,0:T(8,128)} %bitcast.7), custom_call_target="tpu_custom_call" | custom-call | tf_op jit(solution)/shard_map/pallas_call | solution.py:596
  21.6 4.6 %shard_map.69 = (f32[1280,128]{1,0:T(8,128)}, f32[3,5,6,2048]{3,2,1,0:T(8,128)}) custom-call(f32[1280,128]{1,0:T(8,128)} %get-tuple-element.6.updated_in, f32[3,208,128]{2,1,0:T(8,128)S(1)} %get-tuple-element.7.window), custom_call_target="tpu_custom_call" | custom-call | tf_op jit(solution)/shard_map/pallas_call | solution.py:646
Async XLA Ops:
  1.3 0.7 %copy-start = (s32[3,6]{1,0:T(4,128)S(1)}, s32[3,6]{1,0:T(4,128)}, u32[]{:S(2)}) copy-start(s32[3,6]{1,0:T(4,128)} %mask_far.1) | copy-start | bytes 220
  2.0 0.7 %copy-start.1 = (s32[3,2]{0,1:T(2,128)S(1)}, s32[3,2]{0,1:T(2,128)}, u32[]{:S(2)}) copy-start(s32[3,2]{0,1:T(2,128)} %param.7) | copy-start | bytes 76

commit v4 on v3

--- a/solution.py
+++ b/solution.py
@@ -38,10 +38,10 @@
     return jnp.concatenate([table, table], axis=0)
 
 
-def transposed_groups(arrays, edge):
+def transposed_groups(arrays, edge, bits=(4, 2, 1)):
     out = list(arrays)
     group = iota(out[0].shape, 1) // edge
-    for bit in (4, 2, 1):
+    for bit in bits:
         low = (group // bit) % 2 == 0
         for i in range(8):
             if i & bit == 0:
@@ -60,7 +60,7 @@
         self.corner = self.z + self.z_size
         self.own = self.corner + 4
         self.keep = self.own + 12 * fields
-        self.rows = self.keep + 6
+        self.rows = self.keep + 1
         self.rows = self.rows + (-self.rows) % SUB
         self.field = edge * edge + SUB
 
@@ -95,8 +95,8 @@
 
 def kernel(
     n_box, n_lev, slots, fields, edge,
-    owner_far, count_far, mask_far, fine_far, coarse_far, updated, window,
-    owner_of, count, mask, fine, coarse, avg, own_got, send1, recv1, region_out, near_in,
+    owner_far, count_far, fine_far, coarse_far, updated, window,
+    owner_of, count, fine, coarse, avg, own_got, send1, recv1, region_out, near_in,
     upd, corner_lines, corner_region, side_out, side_in, z_out, z_in, corner_out, corner_in, place_table,
     small, load, put, s1, r1, sh, rh, s3, r3, mixed,
 ):
@@ -109,7 +109,7 @@
     chunks = ((0, cut), (cut, fields))
     small_loads = [
         pltpu.make_async_copy(src, dst, small.at[i])
-        for i, (src, dst) in enumerate(((owner_far, owner_of), (count_far, count), (mask_far, mask)))
+        for i, (src, dst) in enumerate(((owner_far, owner_of), (count_far, count)))
     ]
     for copy in small_loads:
         copy.start()
@@ -127,7 +127,7 @@
                 copy.start()
         rows = fine.at[pl.ds(0, 8 * slots * (f1 - f0) * fine_edge)]
         loads[part] = pltpu.make_async_copy(rows, rows, load.at[part])
-    coarse_load = pltpu.make_async_copy(coarse_far, coarse, small.at[3])
+    coarse_load = pltpu.make_async_copy(coarse_far, coarse, small.at[2])
     coarse_load.start()
     n_dev = n_box * n_lev
     offsets, reach, same = relations(n_box, n_lev)
@@ -270,9 +270,8 @@
                 to = lay.own + (2 * (2 + kind) + h) * fields
                 window[s, to:to + fields, :] = total
 
-        for face in range(6):
-            keep = jnp.where((s < live_count) & (mask[s, face] > 0), 1.0, 0.0).astype(F32)
-            window[s, lay.keep + face:lay.keep + face + 1, :] = jnp.full((1, LANES), 1.0, F32) * keep
+        live = jnp.where(s < live_count, 1.0, 0.0).astype(F32)
+        window[s, lay.keep:lay.keep + 1, :] = jnp.full((1, LANES), 1.0, F32) * live
     corner_lines[...] = jnp.zeros_like(corner_lines)
     coarse_load.wait()
     told = near_in.at[pl.ds(0, len(offsets))]
@@ -425,6 +424,14 @@
                     jnp.zeros((4, LANES), F32)
                 )
 
+        if d % 2:
+            for near_d in (d - 1, d):
+                for k in order:
+                    send(
+                        side_out.at[pl.ds((near_d * 4 + k) * lay.side, lay.side)],
+                        side_in.at[k, near_d], 1, near_d, k, targets[near_d][k],
+                    )
+
     for f in range(fields):
         for corner in range(4):
             x = 0 if corner // 2 else edge - 1
@@ -439,12 +446,6 @@
             total = jnp.where(region == float(g), by_region[g], total)
         for corner in range(4):
             corner_out[corner * 4 + k] = total[corner:corner + 1, :]
-    for d in (0, 1, 2, 3):
-        for k in order:
-            send(
-                side_out.at[pl.ds((d * 4 + k) * lay.side, lay.side)], side_in.at[k, d],
-                1, d, k, targets[d][k],
-            )
     for corner in range(4):
         for k in order:
             send(
@@ -475,32 +476,55 @@
 
 
 def ghost_kernel(
-    slots, fields, edge, updated_in, window, updated_out, ghost_out, passing, ghost, lhs, pass_sem, out_sem
+    slots, fields, edge, mask_far, updated_in, window, updated_out, ghost_out,
+    mask, passing, ghost, table, lhs, mask_sem, pass_sem, out_sem,
 ):
     lay = Layout(fields, edge)
     into = pltpu.make_async_copy(updated_in, passing, pass_sem.at[0])
     out = pltpu.make_async_copy(passing, updated_out, pass_sem.at[1])
+    mask_load = pltpu.make_async_copy(mask_far, mask, mask_sem.at[0])
+    mask_load.start()
     into.start()
 
-    def weights(width, target, along, within, normal):
-        row = iota((LANES, width), 0)
-        part = (row // edge) % 4
-        signs = jnp.where(part == 1, along, jnp.where(part == 2, within, normal))
-        value = jnp.where(part == 0, 1.0, jnp.where(signs == 1, 0.125, -0.125))
-        return jnp.where(row % edge == target, value, 0.0).astype(BF16)
-
-    lx = iota((LANES, 2 * LANES), 1)
-    lz = iota((LANES, LANES), 1)
+    table[...] = jnp.zeros_like(table)
+    cell_row = iota((edge, LANES), 0)
+    col = iota((edge, LANES), 1)
     quarter = 2 * edge
-    tables = (
-        weights(2 * LANES, (lx % quarter) // 2, (lx // quarter) % 2, lx % 2, lx // LANES),
-        weights(LANES, (lz % quarter) // 2, lz // 64, lz % 2, (lz // quarter) % 2),
-        weights(LANES, (lz % 64) // 4, lz // 64, (lz // 2) % 2, lz % 2),
-    )
+    for kind in range(3):
+        target = (col % 64) // 4 if kind == 2 else (col % quarter) // 2
+        along = (col // quarter) % 2 if kind == 0 else col // 64
+        within = (col // 2) % 2 if kind == 2 else col % 2
+        step = cell_row - target
+        alike = step == 0
+
+        def signed(sign, where):
+            return jnp.where(where, jnp.where(sign == 1, 0.125, -0.125), 0.0)
+
+        centre = jnp.where(alike, 1.0, signed(within, step == 1) - signed(within, step == -1))
+        ends = signed(within, step == 1 - edge) - signed(within, step == edge - 1)
+        slope = signed(along, alike)
+        for odd in range(2):
+            for line in range(2):
+                block = 2 * odd + line
+                for column in range(2):
+                    if kind == 0:
+                        normal = jnp.where(alike, 0.125 if column else -0.125, 0.0)
+                        used = col // 64 == line
+                    else:
+                        normal = signed(col % 2 if kind == 2 else (col // quarter) % 2, alike)
+                        used = None if column == line else False
+                    if used is False:
+                        continue
+                    for part, value in enumerate((centre, slope, normal, ends)):
+                        if used is not None:
+                            value = jnp.where(used, value, 0.0)
+                        row = (part % 2) * LANES + (odd * 4 + (part // 2) * 2 + line) * edge
+                        to = (2 * odd + column) * LANES
+                        table[kind, row:row + edge, to:to + LANES] = value.astype(BF16)
+
     lane = iota((SUB, LANES), 1)
     in_group = lane % edge
     last_lane, first_lane = lane >= LANES - edge, lane < edge
-    low_half = lane < LANES // 2
 
     for s in range(slots):
         def rows(start, size=SUB):
@@ -511,7 +535,7 @@
             return pltpu.roll(row, shift % LANES, 1, stride=stride, stride_axis=0)
 
         for kind in range(3):
-            parts = [[], [], [], []]
+            parts = [[] for _ in range(8)]
             for side in range(2):
                 face = 2 * kind + side
                 base = face * lay.side if kind < 2 else lay.z + side * 4 * fields
@@ -532,54 +556,46 @@
                     jnp.where(last_lane, up[1], up[0]) - jnp.where(first_lane, below, down[0]),
                     jnp.where(last_lane, above, up[1]) - jnp.where(first_lane, down[0], down[1]),
                 ]
-                within = []
                 for h in range(2):
                     if kind < 2:
-                        before = spread(base + lay.ends + h, 1 - edge, 2)
-                        after = spread(base + lay.ends + h, edge - 1, 2)
+                        before = after = spread(base + lay.ends + h, 0, 2)
                     else:
                         low_row, high_row = 2 * lay.side + lay.ends + h, 3 * lay.side + lay.ends + h
-                        before = spread(low_row, 0 if side else 1 - edge, 2)
-                        after = spread(high_row, edge - 1 if side else 0, 2)
-                    right = jnp.where(in_group == edge - 1, after, pltpu.roll(centre[h], LANES - 1, 1))
-                    left = jnp.where(in_group == 0, before, pltpu.roll(centre[h], 1, 1))
-                    within.append(right - left)
-                normal = [(o - v) if side == 0 else (v - o) for o, v in zip(own, far)]
-                for part, values in zip(parts, (centre, along, within, normal)):
-                    part.extend(values)
-            wide = [jnp.concatenate(part, axis=0) for part in parts]
-            high = [v.astype(BF16).astype(F32) for v in wide]
-            low = [v - u for v, u in zip(wide, high)]
-            groups = transposed_groups(high + low, edge)
-            lhs[s * 3 + kind] = jnp.concatenate(groups, axis=0).astype(BF16)
+                        before = spread(low_row, edge - 1 if side else 0, 2)
+                        after = spread(high_row, 0 if side else 1 - edge, 2)
+                    end = jnp.where(in_group == edge - 1, before, jnp.where(in_group == 0, after, 0.0))
+                    normal = own[h] - far[h] if side == 0 else far[h] - own[h]
+                    for part, values in enumerate((centre[h], along[h], normal, end)):
+                        parts[h * 4 + part].append(values)
+            groups = transposed_groups([jnp.concatenate(v, axis=0) for v in parts], edge, (4, 2))
+            for pair in range(4):
+                high, low = split(jnp.concatenate(groups[2 * pair:2 * pair + 2], axis=1))
+                lhs[s * 3 + kind, pair * 16:(pair + 1) * 16, :] = high
+                lhs[s * 3 + kind, 64 + pair * 16:64 + (pair + 1) * 16, :] = low
 
     into.wait()
     out.start()
+    mask_load.wait()
     for s in range(slots):
+        live = window[s, lay.keep:lay.keep + 1, :]
         for kind in range(3):
-            spreads = jnp.dot(lhs[s * 3 + kind], tables[kind], preferred_element_type=F32)
+            both_parts = jnp.dot(lhs[s * 3 + kind], table[kind], preferred_element_type=F32)
+            spreads = both_parts[:64] + both_parts[64:]
             for side in range(2):
                 face = 2 * kind + side
-                keep = window[s, lay.keep + face:lay.keep + face + 1, :]
-                for h in range(2):
-                    def cell(i):
-                        start = (i * 4 + side * 2 + h) * SUB
-                        return spreads[start:start + SUB, :]
-
-                    if kind == 0:
-                        for t in range(4):
-                            for layer in range(2):
-                                cols = slice(layer * LANES, (layer + 1) * LANES)
-                                value = jnp.where(low_half, cell(2 * t)[:, cols], cell(2 * t + 1)[:, cols])
-                                to = (layer * 8 + h * 4 + t) * LANES
-                                ghost[s, :, face, to:to + LANES] = (value * keep)[:fields]
-                    else:
-                        for i in range(8):
-                            to = (h * 8 + i) * LANES
-                            ghost[s, :, face, to:to + LANES] = (cell(i) * keep)[:fields]
-        pltpu.make_async_copy(ghost.at[s], ghost_out.at[s], out_sem.at[0]).start()
+                keep = live * jnp.where(mask[s, face] > 0, 1.0, 0.0).astype(F32)
+                for pair in range(4):
+                    for block in range(4):
+                        start = pair * 16 + side * SUB
+                        value = spreads[start:start + SUB, block * LANES:(block + 1) * LANES] * keep
+                        h, column = block // 2, block % 2
+                        tile = column * 8 + h * 4 + pair if kind == 0 else h * 8 + pair * 2 + column
+                        ghost[s, :, face, tile * LANES:(tile + 1) * LANES] = value[:fields]
+        pltpu.make_async_copy(
+            ghost.at[s, :, :, pl.ds(0, ghost_out.shape[3])], ghost_out.at[s], out_sem.at[0]
+        ).start()
     out.wait()
-    pltpu.make_async_copy(ghost, ghost_out, out_sem.at[0]).wait()
+    pltpu.make_async_copy(ghost_out, ghost_out, out_sem.at[0]).wait()
 
 
 def body(n_box, n_lev, fine, coarse, owner_map, patch_count, face_mask):
@@ -599,12 +615,11 @@
             flat,
             jax.ShapeDtypeStruct((slots, lay.rows, LANES), F32),
         ),
-        in_specs=[far] * 5,
+        in_specs=[far] * 4,
         out_specs=(far, vmem),
         scratch_shapes=[
             pltpu.SMEM(owner_rows.shape, jnp.int32),
             pltpu.SMEM(patch_count.shape, jnp.int32),
-            pltpu.SMEM(face_mask.shape, jnp.int32),
             pltpu.VMEM((8 * slots * fields * fine_edge, LANES), F32),
             pltpu.VMEM((block * edge, LANES), F32),
             pltpu.VMEM((2 * slots * block, LANES), F32),
@@ -623,7 +638,7 @@
             pltpu.VMEM((16, 1, LANES), F32),
             pltpu.VMEM((16, 1, LANES), F32),
             pltpu.VMEM((4, 2 * LANES, 2 * LANES), BF16),
-            pltpu.SemaphoreType.DMA((4,)),
+            pltpu.SemaphoreType.DMA((3,)),
             pltpu.SemaphoreType.DMA((2,)),
             pltpu.SemaphoreType.DMA((1,)),
             pltpu.SemaphoreType.DMA((1,)),
@@ -638,7 +653,7 @@
             collective_id=0, has_side_effects=True, vmem_limit_bytes=VMEM_FIRST
         ),
     )(
-        owner_rows, patch_count, face_mask,
+        owner_rows, patch_count,
         fine.reshape(slots * fields * fine_edge, fine_edge * fine_edge),
         coarse.reshape(block * edge, LANES),
     )
@@ -646,17 +661,20 @@
     updated, ghost = pl.pallas_call(
         functools.partial(ghost_kernel, slots, fields, edge),
         out_shape=(flat, jax.ShapeDtypeStruct(ghost_shape, F32)),
-        in_specs=[far, vmem],
+        in_specs=[far, far, vmem],
         out_specs=(far, far),
         scratch_shapes=[
+            pltpu.SMEM(face_mask.shape, jnp.int32),
             pltpu.VMEM((block * edge, LANES), F32),
-            pltpu.VMEM(ghost_shape, F32),
-            pltpu.VMEM((3 * slots, 2 * LANES, LANES), BF16),
+            pltpu.VMEM((*ghost_shape[:3], ghost_shape[3] + LANES), F32),
+            pltpu.VMEM((3, 2 * LANES, 4 * LANES), BF16),
+            pltpu.VMEM((3 * slots, LANES, 2 * LANES), BF16),
+            pltpu.SemaphoreType.DMA((1,)),
             pltpu.SemaphoreType.DMA((2,)),
             pltpu.SemaphoreType.DMA((1,)),
         ],
         compiler_params=pltpu.CompilerParams(vmem_limit_bytes=VMEM_SECOND),
-    )(updated, window)
+    )(face_mask, updated, window)
     return updated.reshape(coarse.shape), ghost.transpose(0, 2, 1, 3)
 
 

time: 26.5 us -> 24.9 us (0.940)
  Pallas kernels: 23.6 us -> 22.7 us
  local copies, waits for them, and re-layouts: 1.35 us -> 0.68 us
    pallas_call x1, Pallas kernels: 4.61 us -> 3.61 us  [body(): pl.pallas_call(functools.partial(ghost_kernel, slots, fields, edge), out_...]
    unnamed x4, local copies, waits for them, and re-layouts: 1.35 us -> 0.68 us
where the time goes in v4:
time: 24.9 us; the launch traced here: 24.7 us
  Pallas kernels  22.7 us (91%)
  between operations  1.32 us (5%)
  local copies, waits for them, and re-layouts  0.68 us (3%)
    pallas_call x1, Pallas kernels, body(): pl.pallas_call(functools.partial(kernel, n_box, n_lev, slots, fields, edg...  19.1 us
    pallas_call x1, Pallas kernels, body(): pl.pallas_call(functools.partial(ghost_kernel, slots, fields, edge), out_...  3.61 us
    unnamed x4, local copies, waits for them, and re-layouts  0.68 us

profile of v4, /device:TPU:0, one launch (start us, length us, event | category | flops | bytes accessed | tf_op | source)
XLA Modules:
  0.0 24.7 jit_solution(5831931966930026171)
XLA Ops:
  0.6 0.0 copy-start
  1.3 0.0 copy-start.1
  1.3 0.7 %copy-done.1 = s32[3,2]{0,1:T(2,128)S(1)} copy-done((s32[3,2]{0,1:T(2,128)S(1)}, s32[3,2]{0,1:T(2,128)}, u32[]{:S(2)}) %copy-start.1) | copy-done | bytes 48
  2.0 19.1 %shard_map.68 = (f32[1280,128]{1,0:T(8,128)}, f32[3,208,128]{2,1,0:T(8,128)S(1)}) custom-call(s32[2,3]{1,0:T(2,128)S(1)} %bitcast.5, s32[1]{0:T(128)S(6)} %copy.7.count_far, f32[480,1024]{1,0:T(8,128)} %bitcast.6, f32[1280,128]{1,0:T(8,128)} %bitcast.7), custom_call_target="tpu_custom_call" | custom-call | tf_op jit(solution)/shard_map/pallas_call | solution.py:612
  21.1 0.0 copy-done
  21.1 3.6 %shard_map.69 = (f32[1280,128]{1,0:T(8,128)}, f32[3,5,6,2048]{3,2,1,0:T(8,128)}) custom-call(s32[3,6]{1,0:T(4,128)S(1)} %copy-done, f32[1280,128]{1,0:T(8,128)} %get-tuple-element.6.updated_in, f32[3,208,128]{2,1,0:T(8,128)S(1)} %get-tuple-element.7.window), custom_call_target="tpu_custom_call" | custom-call | tf_op jit(solution)/shard_map/pallas_call | solution.py:661
Async XLA Ops:
  0.6 20.5 %copy-start = (s32[3,6]{1,0:T(4,128)S(1)}, s32[3,6]{1,0:T(4,128)}, u32[]{:S(2)}) copy-start(s32[3,6]{1,0:T(4,128)} %mask_far.1) | copy-start | bytes 220
  1.3 0.7 %copy-start.1 = (s32[3,2]{0,1:T(2,128)S(1)}, s32[3,2]{0,1:T(2,128)}, u32[]{:S(2)}) copy-start(s32[3,2]{0,1:T(2,128)} %param.7) | copy-start | bytes 76

commit v5 on v4

--- a/solution.py
+++ b/solution.py
@@ -97,7 +97,7 @@
     n_box, n_lev, slots, fields, edge,
     owner_far, count_far, fine_far, coarse_far, updated, window,
     owner_of, count, fine, coarse, avg, own_got, send1, recv1, region_out, near_in,
-    upd, corner_lines, corner_region, side_out, side_in, z_out, z_in, corner_out, corner_in, place_table,
+    upd, side_table, corner_lines, corner_region, side_out, side_in, z_out, z_in, corner_out, corner_in, place_table,
     small, load, put, s1, r1, sh, rh, s3, r3, mixed,
 ):
     fine_edge = 2 * edge
@@ -107,6 +107,25 @@
     frows = fields * fine_edge
     cut = (fields + 1) // 2
     chunks = ((0, cut), (cut, fields))
+    n_dev = n_box * n_lev
+    offsets, reach, same = relations(n_box, n_lev)
+    box = lax.axis_index("box")
+    lev = lax.axis_index("lev")
+    me = box * n_lev + lev
+
+    def at(linear):
+        return (lax.div(linear, n_lev), lax.rem(linear, n_lev))
+
+    def shifted(by):
+        return at(lax.rem(me + (by + n_dev), n_dev))
+
+    def beside(dx, dy):
+        return (lax.rem(box + (dx + n_box), n_box), lax.rem(lev + (dy + n_lev), n_lev))
+
+    barrier = pltpu.get_barrier_semaphore()
+    for db, dl in offsets:
+        pl.semaphore_signal(barrier, inc=1, device_id=beside(db, dl), device_id_type=MESH_ID)
+
     small_loads = [
         pltpu.make_async_copy(src, dst, small.at[i])
         for i, (src, dst) in enumerate(((owner_far, owner_of), (count_far, count)))
@@ -129,25 +148,6 @@
         loads[part] = pltpu.make_async_copy(rows, rows, load.at[part])
     coarse_load = pltpu.make_async_copy(coarse_far, coarse, small.at[2])
     coarse_load.start()
-    n_dev = n_box * n_lev
-    offsets, reach, same = relations(n_box, n_lev)
-    box = lax.axis_index("box")
-    lev = lax.axis_index("lev")
-    me = box * n_lev + lev
-
-    def at(linear):
-        return (lax.div(linear, n_lev), lax.rem(linear, n_lev))
-
-    def shifted(by):
-        return at(lax.rem(me + (by + n_dev), n_dev))
-
-    def beside(dx, dy):
-        return (lax.rem(box + (dx + n_box), n_box), lax.rem(lev + (dy + n_lev), n_lev))
-
-    barrier = pltpu.get_barrier_semaphore()
-    for db, dl in offsets:
-        pl.semaphore_signal(barrier, inc=1, device_id=beside(db, dl), device_id_type=MESH_ID)
-
     q = iota((fine_edge * fine_edge, plane), 0)
     c = iota((fine_edge * fine_edge, plane), 1)
     goal = (q // (2 * fine_edge)) * edge + (q % fine_edge) // 2
@@ -211,23 +211,22 @@
                 for s in range(1, slots):
                     total = total + averaged[s] * weight[s][k]
                 send1[k, to:to + size, h * LANES:(h + 1) * LANES] = total
-        if part == 0:
-            pl.semaphore_wait(barrier, len(offsets))
-            for db, dl in offsets:
-                slot = ((reach - db) % n_box) * n_lev + (-dl) % n_lev
-                copy = pltpu.make_async_remote_copy(
-                    src_ref=region_out, dst_ref=near_in.at[slot],
-                    send_sem=sh.at[0], recv_sem=rh.at[0],
-                    device_id=beside(db, dl), device_id_type=MESH_ID,
-                )
-                copy.start()
+
+    pl.semaphore_wait(barrier, len(offsets))
+    for db, dl in offsets:
+        slot = ((reach - db) % n_box) * n_lev + (-dl) % n_lev
+        pltpu.make_async_remote_copy(
+            src_ref=region_out, dst_ref=near_in.at[slot], send_sem=sh.at[0], recv_sem=rh.at[0],
+            device_id=beside(db, dl), device_id_type=MESH_ID,
+        ).start()
+    for part, (f0, f1) in enumerate(chunks):
+        to, size = f0 * edge, (f1 - f0) * edge
         for k in order:
-            copy = pltpu.make_async_remote_copy(
+            pltpu.make_async_remote_copy(
                 src_ref=send1.at[k, pl.ds(to, size)], dst_ref=recv1.at[k, pl.ds(to, size)],
                 send_sem=s1.at[0], recv_sem=r1.at[part],
                 device_id=shifted(DELTAS[k]), device_id_type=MESH_ID,
-            )
-            copy.start()
+            ).start()
         rows = recv1.at[:, pl.ds(to, size)]
         first[part] = pltpu.make_async_copy(rows, rows, r1.at[part])
 
@@ -296,9 +295,39 @@
                 z_rows.append(pick(near[d][k], place))
     z_table = jnp.concatenate(z_rows, axis=0).astype(BF16)
     z_table = jnp.concatenate([z_table, z_table], axis=1)
+    z_cell = iota((LANES, LANES), 0).astype(F32)
+    out_lane = iota((1, LANES), 1)
+    inside = (out_lane % edge).astype(F32)
+    outside = jnp.where(out_lane % 2 == 1, -1, edge).astype(F32)
+    for d in (2, 3):
+        for k in range(4):
+            base = z_cell - edge * near[d][k]
+            found = base == inside
+            t = base - outside
+            past = (t == 0.0) | (t == LANES) | (t == -LANES)
+            for i, hit in enumerate((found, past)):
+                side_table[d - 2, i, :, k * LANES:(k + 1) * LANES] = both(
+                    jnp.where(hit, 1.0, 0.0).astype(BF16)
+                )
     for corner in range(4):
         for k in range(4):
             corner_region[k, corner:corner + 1, :] = near[4 + corner][k]
+
+    def z_fields(f0, f1):
+        for f in range(f0, f1):
+            start = f * lay.field
+            got = times_transposed(z_table, split_lanes(upd[start:start + plane, :]))
+            for depth in range(2):
+                for h in range(2):
+                    z_out[pl.ds((2 * depth + h) * fields + f, 8, stride=4 * fields), :] = got[
+                        depth * 8:(depth + 1) * 8, h * LANES:(h + 1) * LANES
+                    ]
+            high_end = got[16:24, LANES:]
+            if f:
+                high_end = pltpu.roll(high_end, LANES - f * edge, 1)
+            low_end = pltpu.roll(got[24:32, :LANES], LANES - (f + 1) * edge, 1)
+            end_lines[0] = jnp.where(group8 == 7 - f, high_end, end_lines[0])
+            end_lines[1] = jnp.where(group8 == 7 - f, low_end, end_lines[1])
 
     group = (iota((1, LANES), 1) // edge).astype(F32)
     here = [group == region for region in here_rows]
@@ -330,20 +359,8 @@
             pltpu.make_async_copy(
                 upd.at[pl.ds(f * lay.field, plane)], updated.at[pl.ds(f * plane, plane)], put.at[0]
             ).start()
-        for f in range(f0, f1):
-            start = f * lay.field
-            got = times_transposed(z_table, split_lanes(upd[start:start + plane, :]))
-            for depth in range(2):
-                for h in range(2):
-                    z_out[pl.ds((2 * depth + h) * fields + f, 8, stride=4 * fields), :] = got[
-                        depth * 8:(depth + 1) * 8, h * LANES:(h + 1) * LANES
-                    ]
-            high_end = got[16:24, LANES:]
-            if f:
-                high_end = pltpu.roll(high_end, LANES - f * edge, 1)
-            low_end = pltpu.roll(got[24:32, :LANES], LANES - (f + 1) * edge, 1)
-            end_lines[0] = jnp.where(group8 == 7 - f, high_end, end_lines[0])
-            end_lines[1] = jnp.where(group8 == 7 - f, low_end, end_lines[1])
+        if part == 0:
+            z_fields(f0, f1)
 
     clear, unclear = [0, 0, 0], []
 
@@ -368,12 +385,17 @@
             pl.when(jnp.logical_not(itself))(remote.start)
             unclear.append((remote, itself))
 
+    z_fields(*chunks[1])
     for k in order:
         send(z_out.at[pl.ds(k * lay.z_size, lay.z_size)], z_in.at[k], 0, None, k, back[k])
-
     field_step = lay.field
     sublane = iota((SUB, LANES), 0)
     in_group = iota((SUB, LANES), 1) % edge
+    wide_group = iota((4 * SUB, LANES), 1) // edge
+    turned = (iota((SUB, LANES), 1) + 2 * sublane) % LANES
+    end_place = jnp.where(
+        (sublane < fields) & ((turned % edge == 0) | (turned % edge == edge - 1)), turned // edge, -1
+    )
     for d in (0, 1, 2, 3):
         outer, inner = (edge, 1) if d < 2 else (1, edge)
         adjacent = edge - 1 if d % 2 == 0 else 0
@@ -384,34 +406,55 @@
                 upd[pl.ds(level * outer + (h * 8 + i) * inner, SUB, stride=field_step), :]
                 for level in (adjacent, far) for h in range(2)
             ], axis=0))
-        by_region = transposed_groups(lines, edge)
-        ends = []
-        for g in range(8):
-            before = by_region[(g + 7) % 8][:2 * SUB]
-            after = by_region[(g + 1) % 8][:2 * SUB]
-            ends.append(jnp.where(iota((2 * SUB, LANES), 1) % edge == 0, after, before))
+        if d < 2:
+            by_region = transposed_groups(lines, edge)
+            ends = []
+            for g in range(8):
+                before = by_region[(g + 7) % 8][:2 * SUB]
+                after = by_region[(g + 1) % 8][:2 * SUB]
+                ends.append(jnp.where(iota((2 * SUB, LANES), 1) % edge == 0, after, before))
+        else:
+            wide = split_lanes(jnp.concatenate(lines, axis=0))
+            ahead = split_lanes(jnp.concatenate([v[:2 * SUB] for v in lines], axis=0))
+            cells = jnp.dot(wide, side_table[d - 2, 0], preferred_element_type=F32)
+            beyond = jnp.dot(ahead, side_table[d - 2, 1], preferred_element_type=F32)
         for k in range(4):
-            region = near[d][k]
-            total = by_region[0]
-            end = ends[0]
-            for g in range(1, 8):
-                hit = region == float(g)
-                total = jnp.where(hit, by_region[g], total)
-                end = jnp.where(hit, ends[g], end)
+            if d < 2:
+                region = near[d][k]
+                total = by_region[0]
+                end = ends[0]
+                for g in range(1, 8):
+                    hit = region == float(g)
+                    total = jnp.where(hit, by_region[g], total)
+                    end = jnp.where(hit, ends[g], end)
+                single = []
+                for h in range(2):
+                    used = (sublane < fields) & ((in_group == 0) | (in_group == edge - 1))
+                    one = jnp.where(used, end[h * SUB:(h + 1) * SUB, :], 0.0)
+                    moved = one
+                    for f in range(1, fields):
+                        moved = jnp.where(sublane == f, pltpu.roll(one, LANES - 2 * f, 1), moved)
+                    single.append(moved)
+            else:
+                cols = slice(k * LANES, (k + 1) * LANES)
+                total = cells[:4 * SUB, cols]
+                for i in range(1, 8):
+                    total = jnp.where(wide_group == i, cells[i * 4 * SUB:(i + 1) * 4 * SUB, cols], total)
+                single = []
+                for h in range(2):
+                    moved = jnp.zeros((SUB, LANES), F32)
+                    for i in range(8):
+                        start = (2 * i + h) * SUB
+                        moved = jnp.where(end_place == i, beyond[start:start + SUB, cols], moved)
+                    single.append(moved)
             base = (d * 4 + k) * lay.side
             for part in range(4):
                 side_out[base + part * fields:base + (part + 1) * fields, :] = total[
                     part * SUB:part * SUB + fields, :
                 ]
             for h in range(2):
-                used = (sublane < fields) & ((in_group == 0) | (in_group == edge - 1))
-                one = jnp.where(used, end[h * SUB:(h + 1) * SUB, :], 0.0)
-                moved = one
-                for f in range(1, fields):
-                    moved = jnp.where(sublane == f, pltpu.roll(one, LANES - 2 * f, 1), moved)
-                one = moved
                 side_out[base + lay.ends + h:base + lay.ends + h + 1, :] = jnp.sum(
-                    one, axis=0, keepdims=True
+                    single[h], axis=0, keepdims=True
                 )
         if d < 2:
             for e in range(2):
@@ -424,8 +467,8 @@
                     jnp.zeros((4, LANES), F32)
                 )
 
-        if d % 2:
-            for near_d in (d - 1, d):
+        if d == 3:
+            for near_d in range(4):
                 for k in order:
                     send(
                         side_out.at[pl.ds((near_d * 4 + k) * lay.side, lay.side)],
@@ -526,7 +569,7 @@
     in_group = lane % edge
     last_lane, first_lane = lane >= LANES - edge, lane < edge
 
-    for s in range(slots):
+    def gather(s):
         def rows(start, size=SUB):
             return window[s, start:start + size, :]
 
@@ -573,10 +616,7 @@
                 lhs[s * 3 + kind, pair * 16:(pair + 1) * 16, :] = high
                 lhs[s * 3 + kind, 64 + pair * 16:64 + (pair + 1) * 16, :] = low
 
-    into.wait()
-    out.start()
-    mask_load.wait()
-    for s in range(slots):
+    def finish(s):
         live = window[s, lay.keep:lay.keep + 1, :]
         for kind in range(3):
             both_parts = jnp.dot(lhs[s * 3 + kind], table[kind], preferred_element_type=F32)
@@ -591,9 +631,22 @@
                         h, column = block // 2, block % 2
                         tile = column * 8 + h * 4 + pair if kind == 0 else h * 8 + pair * 2 + column
                         ghost[s, :, face, tile * LANES:(tile + 1) * LANES] = value[:fields]
+
+    def send(s):
         pltpu.make_async_copy(
             ghost.at[s, :, :, pl.ds(0, ghost_out.shape[3])], ghost_out.at[s], out_sem.at[0]
         ).start()
+
+    gather(0)
+    mask_load.wait()
+    for s in range(slots):
+        if s + 1 < slots:
+            gather(s + 1)
+        finish(s)
+        send(s)
+        if s == 0:
+            into.wait()
+            out.start()
     out.wait()
     pltpu.make_async_copy(ghost_out, ghost_out, out_sem.at[0]).wait()
 
@@ -629,6 +682,7 @@
             pltpu.VMEM((4, 1, LANES), F32),
             pltpu.VMEM((places, 4, 1, LANES), F32),
             pltpu.VMEM((SUB * lay.field, LANES), F32),
+            pltpu.VMEM((2, 2, 2 * LANES, 4 * LANES), BF16),
             pltpu.VMEM((SUB, SUB, LANES), F32),
             pltpu.VMEM((4, SUB, LANES), F32),
             pltpu.VMEM((16 * lay.side, LANES), F32),

time: 24.9 us -> 23.5 us (0.944)
  Pallas kernels: 22.7 us -> 21.3 us
    pallas_call x1, Pallas kernels: 3.61 us -> 2.56 us  [body(): pl.pallas_call(functools.partial(ghost_kernel, slots, fields, edge), out_...]
    pallas_call x1, Pallas kernels: 19.1 us -> 18.7 us  [body(): pl.pallas_call(functools.partial(kernel, n_box, n_lev, slots, fields, edg...]
where the time goes in v5:
time: 23.5 us; the launch traced here: 23.3 us
  Pallas kernels  21.3 us (91%)
  between operations  1.32 us (6%)
  local copies, waits for them, and re-layouts  0.68 us (3%)
    pallas_call x1, Pallas kernels, body(): pl.pallas_call(functools.partial(kernel, n_box, n_lev, slots, fields, edg...  18.7 us
    pallas_call x1, Pallas kernels, body(): pl.pallas_call(functools.partial(ghost_kernel, slots, fields, edge), out_...  2.56 us
    unnamed x4, local copies, waits for them, and re-layouts  0.68 us

profile of v5, /device:TPU:0, one launch (start us, length us, event | category | flops | bytes accessed | tf_op | source)
XLA Modules:
  0.0 23.3 jit_solution(11002994303974435460)
XLA Ops:
  0.6 0.0 copy-start
  1.3 0.0 copy-start.1
  1.3 0.7 %copy-done.1 = s32[3,2]{0,1:T(2,128)S(1)} copy-done((s32[3,2]{0,1:T(2,128)S(1)}, s32[3,2]{0,1:T(2,128)}, u32[]{:S(2)}) %copy-start.1) | copy-done | bytes 48
  2.0 18.7 %shard_map.68 = (f32[1280,128]{1,0:T(8,128)}, f32[3,208,128]{2,1,0:T(8,128)S(1)}) custom-call(s32[2,3]{1,0:T(2,128)S(1)} %bitcast.5, s32[1]{0:T(128)S(6)} %copy.7.count_far, f32[480,1024]{1,0:T(8,128)} %bitcast.6, f32[1280,128]{1,0:T(8,128)} %bitcast.7), custom_call_target="tpu_custom_call" | custom-call | tf_op jit(solution)/shard_map/pallas_call | solution.py:665
  20.7 0.0 copy-done
  20.7 2.6 %shard_map.69 = (f32[1280,128]{1,0:T(8,128)}, f32[3,5,6,2048]{3,2,1,0:T(8,128)}) custom-call(s32[3,6]{1,0:T(4,128)S(1)} %copy-done, f32[1280,128]{1,0:T(8,128)} %get-tuple-element.6.updated_in, f32[3,208,128]{2,1,0:T(8,128)S(1)} %get-tuple-element.7.window), custom_call_target="tpu_custom_call" | custom-call | tf_op jit(solution)/shard_map/pallas_call | solution.py:715
Async XLA Ops:
  0.6 20.1 %copy-start = (s32[3,6]{1,0:T(4,128)S(1)}, s32[3,6]{1,0:T(4,128)}, u32[]{:S(2)}) copy-start(s32[3,6]{1,0:T(4,128)} %mask_far.1) | copy-start | bytes 220
  1.3 0.7 %copy-start.1 = (s32[3,2]{0,1:T(2,128)S(1)}, s32[3,2]{0,1:T(2,128)}, u32[]{:S(2)}) copy-start(s32[3,2]{0,1:T(2,128)} %param.7) | copy-start | bytes 76

commit v6 on v5

--- a/solution.py
+++ b/solution.py
@@ -70,7 +70,7 @@
 
 def relations(n_box, n_lev):
     n_dev = n_box * n_lev
-    offsets, same = set(), {}
+    offsets, same, counts = set(), {}, (set(), set())
     for me in range(n_dev):
         box, lev = divmod(me, n_lev)
 
@@ -81,6 +81,7 @@
 
         for delta in DELTAS:
             add((me + delta) % n_dev)
+        others = [0, 0]
         for d, (dx, dy) in enumerate(DIRECTIONS):
             owner = ((box - dx) % n_box) * n_lev + (lev - dy) % n_lev
             add(owner)
@@ -88,9 +89,12 @@
                 target = (owner - delta) % n_dev
                 add(target)
                 same.setdefault((d, k), set()).add(target == me)
+                others[d // 4] += target != me
+        for kind in range(2):
+            counts[kind].add(others[kind])
     offsets.discard((0, 0))
     reach = max(min(db, n_box - db) for db, _ in offsets)
-    return sorted(offsets), reach, same
+    return sorted(offsets), reach, same, counts
 
 
 def kernel(
@@ -108,7 +112,7 @@
     cut = (fields + 1) // 2
     chunks = ((0, cut), (cut, fields))
     n_dev = n_box * n_lev
-    offsets, reach, same = relations(n_box, n_lev)
+    offsets, reach, same, counts = relations(n_box, n_lev)
     box = lax.axis_index("box")
     lev = lax.axis_index("lev")
     me = box * n_lev + lev
@@ -363,6 +367,7 @@
             z_fields(f0, f1)
 
     clear, unclear = [0, 0, 0], []
+    steady = [True] + [len(v) == 1 for v in counts]
 
     def send(src, dst, sem, d, k, target):
         kinds = {False} if d is None else same[d, k]
@@ -370,7 +375,7 @@
         if False in kinds:
             remote = pltpu.make_async_remote_copy(
                 src_ref=src, dst_ref=dst, recv_sem=r3.at[sem], device_id=target, device_id_type=MESH_ID,
-                send_sem=s3.at[sem] if len(kinds) == 1 else mixed.at[len(unclear)],
+                send_sem=s3.at[sem] if len(kinds) == 1 or steady[sem] else mixed.at[len(unclear)],
             )
         if True in kinds:
             local = pltpu.make_async_copy(src, dst, r3.at[sem])
@@ -383,7 +388,8 @@
             itself = (target[0] == box) & (target[1] == lev)
             pl.when(itself)(local.start)
             pl.when(jnp.logical_not(itself))(remote.start)
-            unclear.append((remote, itself))
+            if not steady[sem]:
+                unclear.append((remote, itself))
 
     z_fields(*chunks[1])
     for k in order:
@@ -510,6 +516,9 @@
     pltpu.make_async_copy(send1, send1, s1.at[0]).wait()
     told = near_in.at[pl.ds(0, len(offsets))]
     pltpu.make_async_copy(told, told, sh.at[0]).wait()
+    for sem in (1, 2):
+        if steady[sem]:
+            clear[sem] = min(counts[sem - 1])
     for sem, (ref, size) in enumerate(((z_out, lay.z_size), (side_out, lay.side), (corner_out, 1))):
         if clear[sem]:
             rows = ref.at[pl.ds(0, clear[sem] * size)]
@@ -633,9 +642,10 @@
                         ghost[s, :, face, tile * LANES:(tile + 1) * LANES] = value[:fields]
 
     def send(s):
-        pltpu.make_async_copy(
-            ghost.at[s, :, :, pl.ds(0, ghost_out.shape[3])], ghost_out.at[s], out_sem.at[0]
-        ).start()
+        for f in range(fields):
+            pltpu.make_async_copy(
+                ghost.at[s, f, :, pl.ds(0, ghost_out.shape[3])], ghost_out.at[s, f], out_sem.at[0]
+            ).start()
 
     gather(0)
     mask_load.wait()
@@ -656,11 +666,12 @@
     edge = fine_edge // 2
     block = fields * edge
     lay = Layout(fields, edge)
-    offsets, reach, same = relations(n_box, n_lev)
+    offsets, reach, same, counts = relations(n_box, n_lev)
     far = pl.BlockSpec(memory_space=pl.ANY)
     vmem = pl.BlockSpec(memory_space=pltpu.VMEM)
     flat = jax.ShapeDtypeStruct((block * edge, LANES), F32)
     places = (2 * reach + 1) * n_lev
+    unsteady = 1 if max(len(v) for v in counts) == 1 else sum(len(v) > 1 for v in same.values())
     owner_rows = owner_map.T
     updated, window = pl.pallas_call(
         functools.partial(kernel, n_box, n_lev, slots, fields, edge),
@@ -701,7 +712,7 @@
             pltpu.SemaphoreType.DMA((1,)),
             pltpu.SemaphoreType.DMA((3,)),
             pltpu.SemaphoreType.DMA((3,)),
-            pltpu.SemaphoreType.DMA((max(1, sum(len(v) > 1 for v in same.values())),)),
+            pltpu.SemaphoreType.DMA((unsteady,)),
         ],
         compiler_params=pltpu.CompilerParams(
             collective_id=0, has_side_effects=True, vmem_limit_bytes=VMEM_FIRST

time: 23.5 us -> 23.4 us (level)
  no operation moved by 1% of the time
where the time goes in v6:
time: 23.4 us; the launch traced here: 23.2 us
  Pallas kernels  21.2 us (91%)
  between operations  1.32 us (6%)
  local copies, waits for them, and re-layouts  0.68 us (3%)
    pallas_call x1, Pallas kernels, body(): pl.pallas_call(functools.partial(kernel, n_box, n_lev, slots, fields, edg...  18.6 us
    pallas_call x1, Pallas kernels, body(): pl.pallas_call(functools.partial(ghost_kernel, slots, fields, edge), out_...  2.56 us
    unnamed x4, local copies, waits for them, and re-layouts  0.68 us

profile of v6, /device:TPU:0, one launch (start us, length us, event | category | flops | bytes accessed | tf_op | source)
XLA Modules:
  0.0 23.2 jit_solution(9089771757118005236)
XLA Ops:
  0.6 0.0 copy-start
  1.3 0.0 copy-start.1
  1.3 0.7 %copy-done.1 = s32[3,2]{0,1:T(2,128)S(1)} copy-done((s32[3,2]{0,1:T(2,128)S(1)}, s32[3,2]{0,1:T(2,128)}, u32[]{:S(2)}) %copy-start.1) | copy-done | bytes 48
  2.0 18.6 %shard_map.68 = (f32[1280,128]{1,0:T(8,128)}, f32[3,208,128]{2,1,0:T(8,128)S(1)}) custom-call(s32[2,3]{1,0:T(2,128)S(1)} %bitcast.5, s32[1]{0:T(128)S(6)} %copy.7.count_far, f32[480,1024]{1,0:T(8,128)} %bitcast.6, f32[1280,128]{1,0:T(8,128)} %bitcast.7), custom_call_target="tpu_custom_call" | custom-call | tf_op jit(solution)/shard_map/pallas_call | solution.py:676
  20.6 0.0 copy-done
  20.6 2.6 %shard_map.69 = (f32[1280,128]{1,0:T(8,128)}, f32[3,5,6,2048]{3,2,1,0:T(8,128)}) custom-call(s32[3,6]{1,0:T(4,128)S(1)} %copy-done, f32[1280,128]{1,0:T(8,128)} %get-tuple-element.6.updated_in, f32[3,208,128]{2,1,0:T(8,128)S(1)} %get-tuple-element.7.window), custom_call_target="tpu_custom_call" | custom-call | tf_op jit(solution)/shard_map/pallas_call | solution.py:726
Async XLA Ops:
  0.6 20.0 %copy-start = (s32[3,6]{1,0:T(4,128)S(1)}, s32[3,6]{1,0:T(4,128)}, u32[]{:S(2)}) copy-start(s32[3,6]{1,0:T(4,128)} %mask_far.1) | copy-start | bytes 220
  1.3 0.7 %copy-start.1 = (s32[3,2]{0,1:T(2,128)S(1)}, s32[3,2]{0,1:T(2,128)}, u32[]{:S(2)}) copy-start(s32[3,2]{0,1:T(2,128)} %param.7) | copy-start | bytes 76

commit v7 on v6

--- a/solution.py
+++ b/solution.py
@@ -299,20 +299,6 @@
                 z_rows.append(pick(near[d][k], place))
     z_table = jnp.concatenate(z_rows, axis=0).astype(BF16)
     z_table = jnp.concatenate([z_table, z_table], axis=1)
-    z_cell = iota((LANES, LANES), 0).astype(F32)
-    out_lane = iota((1, LANES), 1)
-    inside = (out_lane % edge).astype(F32)
-    outside = jnp.where(out_lane % 2 == 1, -1, edge).astype(F32)
-    for d in (2, 3):
-        for k in range(4):
-            base = z_cell - edge * near[d][k]
-            found = base == inside
-            t = base - outside
-            past = (t == 0.0) | (t == LANES) | (t == -LANES)
-            for i, hit in enumerate((found, past)):
-                side_table[d - 2, i, :, k * LANES:(k + 1) * LANES] = both(
-                    jnp.where(hit, 1.0, 0.0).astype(BF16)
-                )
     for corner in range(4):
         for k in range(4):
             corner_region[k, corner:corner + 1, :] = near[4 + corner][k]
@@ -365,6 +351,20 @@
             ).start()
         if part == 0:
             z_fields(f0, f1)
+            z_cell = iota((LANES, LANES), 0).astype(F32)
+            out_lane = iota((1, LANES), 1)
+            inside = (out_lane % edge).astype(F32)
+            outside = jnp.where(out_lane % 2 == 1, -1, edge).astype(F32)
+            for d in (2, 3):
+                for k in range(4):
+                    base = z_cell - edge * near[d][k]
+                    found = base == inside
+                    t = base - outside
+                    past = (t == 0.0) | (t == LANES) | (t == -LANES)
+                    for i, hit in enumerate((found, past)):
+                        side_table[d - 2, i, :, k * LANES:(k + 1) * LANES] = both(
+                            jnp.where(hit, 1.0, 0.0).astype(BF16)
+                        )
 
     clear, unclear = [0, 0, 0], []
     steady = [True] + [len(v) == 1 for v in counts]

time: 23.4 us -> 23.6 us (level)
  no operation moved by 1% of the time
where the time goes in v7:
time: 23.6 us; the launch traced here: 23.3 us
  Pallas kernels  21.3 us (90%)
  between operations  1.32 us (6%)
  local copies, waits for them, and re-layouts  0.68 us (3%)
    pallas_call x1, Pallas kernels, body(): pl.pallas_call(functools.partial(kernel, n_box, n_lev, slots, fields, edg...  18.8 us
    pallas_call x1, Pallas kernels, body(): pl.pallas_call(functools.partial(ghost_kernel, slots, fields, edge), out_...  2.56 us
    unnamed x4, local copies, waits for them, and re-layouts  0.68 us

profile of v7, /device:TPU:0, one launch (start us, length us, event | category | flops | bytes accessed | tf_op | source)
XLA Modules:
  0.0 23.3 jit_solution(9061763941723783279)
XLA Ops:
  0.6 0.0 copy-start
  1.3 0.0 copy-start.1
  1.3 0.7 %copy-done.1 = s32[3,2]{0,1:T(2,128)S(1)} copy-done((s32[3,2]{0,1:T(2,128)S(1)}, s32[3,2]{0,1:T(2,128)}, u32[]{:S(2)}) %copy-start.1) | copy-done | bytes 48
  2.0 18.8 %shard_map.68 = (f32[1280,128]{1,0:T(8,128)}, f32[3,208,128]{2,1,0:T(8,128)S(1)}) custom-call(s32[2,3]{1,0:T(2,128)S(1)} %bitcast.5, s32[1]{0:T(128)S(6)} %copy.7.count_far, f32[480,1024]{1,0:T(8,128)} %bitcast.6, f32[1280,128]{1,0:T(8,128)} %bitcast.7), custom_call_target="tpu_custom_call" | custom-call | tf_op jit(solution)/shard_map/pallas_call | solution.py:676
  20.8 0.0 copy-done
  20.8 2.6 %shard_map.69 = (f32[1280,128]{1,0:T(8,128)}, f32[3,5,6,2048]{3,2,1,0:T(8,128)}) custom-call(s32[3,6]{1,0:T(4,128)S(1)} %copy-done, f32[1280,128]{1,0:T(8,128)} %get-tuple-element.6.updated_in, f32[3,208,128]{2,1,0:T(8,128)S(1)} %get-tuple-element.7.window), custom_call_target="tpu_custom_call" | custom-call | tf_op jit(solution)/shard_map/pallas_call | solution.py:726
Async XLA Ops:
  0.6 20.1 %copy-start = (s32[3,6]{1,0:T(4,128)S(1)}, s32[3,6]{1,0:T(4,128)}, u32[]{:S(2)}) copy-start(s32[3,6]{1,0:T(4,128)} %mask_far.1) | copy-start | bytes 220
  1.3 0.7 %copy-start.1 = (s32[3,2]{0,1:T(2,128)S(1)}, s32[3,2]{0,1:T(2,128)}, u32[]{:S(2)}) copy-start(s32[3,2]{0,1:T(2,128)} %param.7) | copy-start | bytes 76
